TPU v7x, 128 devices: a whole 4x4x4 slice. The times are simulated.
128 devices in a mesh: ty: 8 (over y, core), tx: 16 (over x, z).
Axes of the slice: x: 4, y: 4, z: 4, core: 2. Of those that a mesh axis runs over, the one named last changes fastest.
Arguments:
- node_state: bfloat16 [8192, 256], P(('ty', 'tx')), may hold values from -6 to 6
- edge_state: bfloat16 [8192, 50, 256], P(('ty', 'tx')), may hold values from -6 to 6
- noisy_edges: float32 [8192, 50], P(('ty', 'tx')), may hold values from -1 to 1
- timestep: int32 [1], replicated, may hold values from 1 to 999
- neighbors: int32 [8192, 50], P(('ty', 'tx')), may hold values from -1 to 8191, as said below
- mirror_src: int32 [8192, 50], P(('ty', 'tx')), may hold values from -1 to 3327, as said below
- send_rows: int32 [128, 8, 16], P(('ty', 'tx')), may hold values from -1 to 3199, as said below
- node_own: bfloat16 [3, 256, 512], replicated, may hold values from -0.375 to 0.375
- node_nbr: bfloat16 [3, 256, 512], replicated, may hold values from -0.375 to 0.375
- edge_weight: bfloat16 [3, 256, 256], replicated, may hold values from -0.375 to 0.375
- noise_embed: float32 [256], replicated, may hold values from -6 to 6
- time_embed: float32 [256, 256], replicated, may hold values from -0.375 to 0.375
- time_layer: float32 [3, 256, 256], replicated, may hold values from -0.375 to 0.375
Outputs:
- node_out: bfloat16 [8192, 256], P(('ty', 'tx'))
- edge_out: bfloat16 [8192, 50, 256], P(('ty', 'tx'))
Inputs may be any that keep to these rules, and one draw needn't show every extreme that they name: `neighbors`: every listed neighbour lies in the city's own tile or one of the 8 tiles adjacent to it (diagonals too); padding slots hold -1. mirror_src[i, k] is -1 or an index of lookup (the tile's own edge rows, then incoming); the row it names is the edge from neighbors[i, k] back to city i. An index of 3200 or more, d * 16 + p past the own rows, names the p-th row from offset d. send_rows[s, d] lists, -1 for unused entries, the rows of tile s that the tile at offset minus d from s reads as its offset d rows, in order; at most 16 rows for one pair of adjacent tiles, and in every draw some tile reads exactly 16 from each adjacent tile and they from it.
All inputs are finite; a program needn't handle non-finite values.
Results may differ from a plain program's by a relative error of at most 0.0055.
Values may be sent and summed in bfloat16 or wider, within the bound.
A program may use at most 64 MiB of HBM per device.

v0:
```python
import math

import jax
import jax.numpy as jnp
from jax import lax
from jax.sharding import PartitionSpec as P

LAYERS = 3


def extended(value, sides, width):
    for axis, dim in sides:
        peers, length = (lax.axis_size(axis), value.shape[dim])
        up = [(i, (i + 1) % peers) for i in range(peers - 1)]
        down = [(j, i) for i, j in up]
        last = lax.slice_in_dim(value, length - width, length, axis=dim)
        first = lax.slice_in_dim(value, 0, width, axis=dim)
        before = lax.ppermute(last, axis, up)
        after = lax.ppermute(first, axis, down)
        value = jnp.concatenate([before, value, after], axis=dim)
    return value


def from_behind(block, axis, distance):
    devices = range(lax.axis_size(axis))
    route = [(i - distance, i) for i in devices if i - distance in devices]
    return lax.ppermute(block, axis, route)


def direction_list():
    return [
        (step_y, step_x)
        for step_y in (-1, 0, 1)
        for step_x in (-1, 0, 1)
        if step_y != 0 or step_x != 0
    ]


def layer_norm(values):
    centered = values - jnp.mean(values, axis=-1, keepdims=True)
    spread = jnp.mean(centered * centered, axis=-1, keepdims=True)
    return centered * lax.rsqrt(spread + 1e-05)


def time_hidden_of(timestep, time_embed):
    features = time_embed.shape[0]
    half_width = features // 2
    frequency = jnp.exp(-math.log(10000.0) * jnp.arange(half_width, dtype=jnp.float32) / half_width)
    phases = timestep[0].astype(jnp.float32) * frequency
    embedding = jnp.concatenate([jnp.cos(phases), jnp.sin(phases)])[None, :]
    return jax.nn.relu(jnp.dot(embedding, time_embed, precision=lax.Precision.HIGHEST))


def edge_update(
    node_rows, averaged, own_proj, picked, is_valid, noisy, noise_embed, time_row, weight
):
    cities = picked.shape[0]
    slot_count = picked.shape[1]
    features = averaged.shape[1]
    valid3 = is_valid[:, :, None]
    mixed_rows = jnp.dot(averaged, weight, preferred_element_type=jnp.float32).reshape(
        cities, slot_count, features
    )
    picked_src = picked[:, :, :features].astype(jnp.float32)
    picked_msg = picked[:, :, features:].astype(jnp.float32)
    pre_gate = mixed_rows + own_proj[:, None, :features] + jnp.where(valid3, picked_src, 0.0)
    pre_gate = pre_gate + noisy[:, :, None] * noise_embed + time_row
    gate_vals = jnp.where(valid3, jax.nn.sigmoid(pre_gate), 0.0)
    gathered = jnp.sum(gate_vals * picked_msg, axis=1)
    node_next = (
        node_rows.astype(jnp.float32) + jax.nn.relu(layer_norm(own_proj[:, features:] + gathered))
    ).astype(jnp.bfloat16)
    averaged3 = averaged.reshape(cities, slot_count, features).astype(jnp.float32)
    edge_next = jnp.where(valid3, averaged3 + jax.nn.relu(layer_norm(pre_gate)), 0.0).astype(
        jnp.bfloat16
    )
    return (node_next, edge_next)


def on_device(
    node_state,
    edge_state,
    noisy_edges,
    timestep,
    neighbors,
    mirror_src,
    send_rows,
    node_own,
    node_nbr,
    edge_weight,
    noise_embed,
    time_embed,
    time_layer,
):
    cities = node_state.shape[0]
    features = node_state.shape[1]
    slot_count = edge_state.shape[1]
    row_count = cities * slot_count
    capacity = send_rows.shape[2]
    directions = direction_list()
    grid_x = lax.axis_size("tx")
    here_y = lax.axis_index("ty")
    here_x = lax.axis_index("tx")
    is_valid = neighbors >= 0
    safe_nbr = jnp.where(is_valid, neighbors, 0)
    tile_of = safe_nbr // cities
    rel_y = tile_of // grid_x - here_y + 1
    rel_x = tile_of % grid_x - here_x + 1
    source_rows = jnp.where(
        is_valid, (rel_y * 3 + rel_x) * cities + safe_nbr % cities, 4 * cities
    ).reshape(-1)
    send_live = send_rows[0] >= 0
    send_safe = jnp.maximum(send_rows[0], 0).reshape(-1)
    has_mirror = (mirror_src >= 0).reshape(row_count, 1)
    partner_rows = jnp.maximum(mirror_src, 0).reshape(-1)
    hidden_time = time_hidden_of(timestep, time_embed)
    node_rows = node_state
    edge_rows = edge_state.reshape(row_count, features)
    for layer_at in range(LAYERS):
        time_row = jnp.dot(hidden_time, time_layer[layer_at], precision=lax.Precision.HIGHEST)
        fetched = jnp.take(edge_rows, send_safe, axis=0).reshape(8, capacity, features)
        outgoing = jnp.where(send_live[:, :, None], fetched, jnp.zeros_like(fetched))
        own_proj = jnp.dot(node_rows, node_own[layer_at], preferred_element_type=jnp.float32)
        node_payload = node_rows
        payload_width = node_payload.shape[1]
        beside_all = extended(node_payload[None, None], (("ty", 0), ("tx", 1)), 1)
        tile_rows = beside_all.reshape(9 * cities, payload_width)
        arrived = []
        for direction, (step_y, step_x) in enumerate(directions):
            buffer_rows = outgoing[direction]
            if step_y != 0:
                buffer_rows = from_behind(buffer_rows, "ty", -step_y)
            if step_x != 0:
                buffer_rows = from_behind(buffer_rows, "tx", -step_x)
            arrived.append(buffer_rows)
        incoming = jnp.stack(arrived).reshape(8 * capacity, features)
        nbr_proj = jnp.dot(
            tile_rows, node_nbr[layer_at], preferred_element_type=jnp.float32
        ).astype(jnp.bfloat16)
        picked = jnp.take(nbr_proj, source_rows, axis=0).reshape(cities, slot_count, 2 * features)
        lookup = jnp.concatenate([edge_rows, incoming], axis=0)
        partner = jnp.take(lookup, partner_rows, axis=0)
        averaged = jnp.where(
            has_mirror,
            (edge_rows.astype(jnp.float32) + partner.astype(jnp.float32)) * 0.5,
            edge_rows.astype(jnp.float32),
        ).astype(jnp.bfloat16)
        node_rows, edge_next = edge_update(
            node_rows,
            averaged,
            own_proj,
            picked,
            is_valid,
            noisy_edges,
            noise_embed,
            time_row,
            edge_weight[layer_at],
        )
        edge_rows = edge_next.reshape(row_count, features)
    return (node_rows, edge_rows.reshape(cities, slot_count, features))


def solution(mesh):
    return jax.shard_map(
        on_device,
        mesh=mesh,
        in_specs=(
            P(("ty", "tx"), None),
            P(("ty", "tx"), None, None),
            P(("ty", "tx"), None),
            P(),
            P(("ty", "tx"), None),
            P(("ty", "tx"), None),
            P(("ty", "tx"), None, None),
            P(),
            P(),
            P(),
            P(),
            P(),
            P(),
        ),
        out_specs=(P(("ty", "tx"), None), P(("ty", "tx"), None, None)),
        check_vma=False,
    )
```

profile of v0, /device:TPU:22, one launch (start us, length us, event | category | flops | bytes accessed | tf_op | source)
XLA Modules:
  0.0 334.3 jit_solution(14531141641364040297)
XLA Ops:
  2.7 3.6 %collective-permute-start.13 = (bf16[1,1,64,256]{3,2,1,0:T(8,128)(2,1)}, bf16[1,1,64,256]{3,2,1,0:T(8,128)(2,1)}, u32[]{:S(2)}, u32[]{:S(2)}) collective-permute-start(bf16[1,1,64,256]{3,2,1,0:T(8,128)(2,1)} %bitcast.187), channel_id=1, source_target_pairs={{16,0},{32,16},{48,32},{64,48},{80,64},{96,80},{112,96},{17,1},{33... | collective-permute-start | bytes 98312 | tf_op jit(solution)/shard_map/ppermute | solution.py:19
  7.9 3.6 %copy.17 = bf16[64,50,256]{2,1,0:T(8,128)(2,1)} copy(bf16[64,50,256]{2,0,1:T(8,128)(2,1)} %param.20) | data formatting | bytes 3276800 | tf_op args[1]
  17.1 3.3 collective-permute-start.2
  28.1 3.8 %collective-permute-start.1 = (bf16[16,256]{1,0:T(8,128)(2,1)S(1)}, bf16[16,256]{1,0:T(8,128)(2,1)S(1)}, u32[]{:S(2)}, u32[]{:S(2)}) collective-permute-start(bf16[16,256]{1,0:T(8,128)(2,1)S(1)} %collective-permute-done), channel_id=1, source_target_pairs={{0,1},{1,2},{2,3},{3,4},{4,5},{5,6},{6,7},{7,8},{8,9},{9,10},{10,1... | collective-permute-start | bytes 24584 | tf_op jit(solution)/shard_map/ppermute | solution.py:27
  32.2 3.7 %collective-permute-done.1 = bf16[16,256]{1,0:T(8,128)(2,1)S(1)} collective-permute-done((bf16[16,256]{1,0:T(8,128)(2,1)S(1)}, bf16[16,256]{1,0:T(8,128)(2,1)S(1)}, u32[]{:S(2)}, u32[]{:S(2)}) %collective-permute-start.1) | collective-permute-done | bytes 8224 | tf_op jit(solution)/shard_map/ppermute | solution.py:27
  37.8 6.0 %collective-permute-start.6 = (bf16[16,256]{1,0:T(8,128)(2,1)S(1)}, bf16[16,256]{1,0:T(8,128)(2,1)S(1)}, u32[]{:S(2)}, u32[]{:S(2)}) collective-permute-start(bf16[16,256]{1,0:T(8,128)(2,1)S(1)} %get-tuple-element.36), channel_id=1, source_target_pairs={{1,0},{2,1},{3,2},{4,3},{5,4},{6,5},{7,6},{8,7},{9,8},{10,9},{11,1... | collective-permute-start | bytes 24584 | tf_op jit(solution)/shard_map/ppermute | solution.py:27
  45.8 3.6 %collective-permute-done.4 = bf16[16,256]{1,0:T(8,128)(2,1)S(1)} collective-permute-done((bf16[16,256]{1,0:T(8,128)(2,1)S(1)}, bf16[16,256]{1,0:T(8,128)(2,1)S(1)}, u32[]{:S(2)}, u32[]{:S(2)}) %collective-permute-start.4) | collective-permute-done | bytes 8224 | tf_op jit(solution)/shard_map/ppermute | solution.py:27
  58.0 6.0 %collective-permute-start.11 = (bf16[16,256]{1,0:T(8,128)(2,1)S(1)}, bf16[16,256]{1,0:T(8,128)(2,1)S(1)}, u32[]{:S(2)}, u32[]{:S(2)}) collective-permute-start(bf16[16,256]{1,0:T(8,128)(2,1)S(1)} %collective-permute-done.10), channel_id=1, source_target_pairs={{1,0},{2,1},{3,2},{4,3},{5,4},{6,5},{7,6},{8,7},{9,8},{10,9},{11,1... | collective-permute-start | bytes 24584 | tf_op jit(solution)/shard_map/ppermute | solution.py:27
  65.5 10.2 %gather_fusion.1 = bf16[3200,256]{1,0:T(8,128)(2,1)} fusion(bf16[3328,256]{1,0:T(8,128)(2,1)S(1)} %pad_maximum_fusion, s32[4096]{0:T(1024)S(1)} %get-tuple-element.50), kind=kCustom, calls=%fused_computation.1.clone | custom fusion | bytes 3289600 | tf_op jit(solution)/shard_map/jit(_take)/gather | solution.py:142
  79.1 6.5 %collective-permute-start.15 = (bf16[3,1,64,256]{3,2,1,0:T(8,128)(2,1)}, bf16[3,1,64,256]{3,2,1,0:T(8,128)(2,1)}, u32[]{:S(2)}, u32[]{:S(2)}) collective-permute-start(bf16[3,1,64,256]{3,2,1,0:T(8,128)(2,1)} %pad_maximum_fusion.6), channel_id=1, source_target_pairs={{1,0},{2,1},{3,2},{4,3},{5,4},{6,5},{7,6},{8,7},{9,8},{10,9},{11,1... | collective-permute-start | bytes 294920 | tf_op jit(solution)/shard_map/ppermute | solution.py:19
  85.6 4.4 %fusion.1 = bf16[3200,256]{1,0:T(8,128)(2,1)S(1)} fusion(bf16[3200,256]{1,0:T(8,128)(2,1)S(1)} %reshape.190, bf16[3200,256]{1,0:T(8,128)(2,1)} %gather_fusion.1, pred[3200]{0:T(1024)(128)(4,1)S(1)} %compare_and_fusion.1, pred[3200]{0:T(1024)(128)(4,1)S(1)} %broadcast_in_dim.147), kind=kLoop, calls=%fused_computation.19 | loop fusion | flops 5734400 | bytes 4921600 | tf_op jit(solution)/shard_map/convert_element_type | solution.py:147
  93.7 10.3 %gather_fusion.2 = bf16[3200,512]{1,0:T(8,128)(2,1)} fusion(bf16[576,512]{1,0:T(8,128)(2,1)S(1)} %convolution_convert_fusion.2, s32[4096]{0:T(1024)S(1)} %get-tuple-element.49), kind=kCustom, calls=%fused_computation.2.clone | custom fusion | bytes 6566400 | tf_op jit(solution)/shard_map/jit(_take)/gather | solution.py:140
  104.0 3.1 broadcast_select_fusion.2
  127.9 3.3 collective-permute-start.28
  138.6 3.2 collective-permute-start.19
  143.7 6.0 %collective-permute-start.22 = (bf16[16,256]{1,0:T(8,128)(2,1)S(1)}, bf16[16,256]{1,0:T(8,128)(2,1)S(1)}, u32[]{:S(2)}, u32[]{:S(2)}) collective-permute-start(bf16[16,256]{1,0:T(8,128)(2,1)S(1)} %get-tuple-element.28), channel_id=1, source_target_pairs={{1,0},{2,1},{3,2},{4,3},{5,4},{6,5},{7,6},{8,7},{9,8},{10,9},{11,1... | collective-permute-start | bytes 24584 | tf_op jit(solution)/shard_map/ppermute | solution.py:27
  149.8 3.9 %collective-permute-start.20 = (bf16[16,256]{1,0:T(8,128)(2,1)S(1)}, bf16[16,256]{1,0:T(8,128)(2,1)S(1)}, u32[]{:S(2)}, u32[]{:S(2)}) collective-permute-start(bf16[16,256]{1,0:T(8,128)(2,1)S(1)} %collective-permute-done.19), channel_id=1, source_target_pairs={{1,0},{2,1},{3,2},{4,3},{5,4},{6,5},{7,6},{8,7},{9,8},{10,9},{11,1... | collective-permute-start | bytes 24584 | tf_op jit(solution)/shard_map/ppermute | solution.py:27
  163.9 6.0 %collective-permute-start.27 = (bf16[16,256]{1,0:T(8,128)(2,1)S(1)}, bf16[16,256]{1,0:T(8,128)(2,1)S(1)}, u32[]{:S(2)}, u32[]{:S(2)}) collective-permute-start(bf16[16,256]{1,0:T(8,128)(2,1)S(1)} %collective-permute-done.26), channel_id=1, source_target_pairs={{1,0},{2,1},{3,2},{4,3},{5,4},{6,5},{7,6},{8,7},{9,8},{10,9},{11,1... | collective-permute-start | bytes 24584 | tf_op jit(solution)/shard_map/ppermute | solution.py:27
  171.4 10.4 %gather_fusion.4 = bf16[3200,256]{1,0:T(8,128)(2,1)} fusion(bf16[3328,256]{1,0:T(8,128)(2,1)S(1)} %pad_maximum_fusion.1, s32[4096]{0:T(1024)} %copy-done.16), kind=kCustom, calls=%fused_computation.5.clone | custom fusion | bytes 3289600 | tf_op jit(solution)/shard_map/jit(_take)/gather | solution.py:142
  185.2 6.5 %collective-permute-start.31 = (bf16[3,1,64,256]{3,2,1,0:T(8,128)(2,1)}, bf16[3,1,64,256]{3,2,1,0:T(8,128)(2,1)}, u32[]{:S(2)}, u32[]{:S(2)}) collective-permute-start(bf16[3,1,64,256]{3,2,1,0:T(8,128)(2,1)} %pad_maximum_fusion.7), channel_id=1, source_target_pairs={{1,0},{2,1},{3,2},{4,3},{5,4},{6,5},{7,6},{8,7},{9,8},{10,9},{11,1... | collective-permute-start | bytes 294920 | tf_op jit(solution)/shard_map/ppermute | solution.py:19
  191.7 4.4 %fusion.3 = bf16[3200,256]{1,0:T(8,128)(2,1)S(1)} fusion(bf16[3200,256]{1,0:T(8,128)(2,1)S(1)} %reshape.197, bf16[3200,256]{1,0:T(8,128)(2,1)} %gather_fusion.4, pred[3200]{0:T(1024)(128)(4,1)S(1)} %compare_and_fusion.1, pred[3200]{0:T(1024)(128)(4,1)S(1)} %broadcast_in_dim.147), kind=kLoop, calls=%fused_computation.21 | loop fusion | flops 5734400 | bytes 4921600 | tf_op jit(solution)/shard_map/convert_element_type | solution.py:147
  199.9 10.3 %gather_fusion.5 = bf16[3200,512]{1,0:T(8,128)(2,1)} fusion(bf16[576,512]{1,0:T(8,128)(2,1)S(1)} %convolution_convert_fusion.1, s32[4096]{0:T(1024)S(1)} %copy-done.14), kind=kCustom, calls=%fused_computation.7.clone | custom fusion | bytes 6566400 | tf_op jit(solution)/shard_map/jit(_take)/gather | solution.py:140
  234.0 3.3 collective-permute-start.44
  244.7 3.2 collective-permute-start.35
  249.9 6.0 %collective-permute-start.38 = (bf16[16,256]{1,0:T(8,128)(2,1)S(1)}, bf16[16,256]{1,0:T(8,128)(2,1)S(1)}, u32[]{:S(2)}, u32[]{:S(2)}) collective-permute-start(bf16[16,256]{1,0:T(8,128)(2,1)S(1)} %get-tuple-element.20), channel_id=1, source_target_pairs={{1,0},{2,1},{3,2},{4,3},{5,4},{6,5},{7,6},{8,7},{9,8},{10,9},{11,1... | collective-permute-start | bytes 24584 | tf_op jit(solution)/shard_map/ppermute | solution.py:27
  255.9 3.9 %collective-permute-start.36 = (bf16[16,256]{1,0:T(8,128)(2,1)S(1)}, bf16[16,256]{1,0:T(8,128)(2,1)S(1)}, u32[]{:S(2)}, u32[]{:S(2)}) collective-permute-start(bf16[16,256]{1,0:T(8,128)(2,1)S(1)} %collective-permute-done.35), channel_id=1, source_target_pairs={{1,0},{2,1},{3,2},{4,3},{5,4},{6,5},{7,6},{8,7},{9,8},{10,9},{11,1... | collective-permute-start | bytes 24584 | tf_op jit(solution)/shard_map/ppermute | solution.py:27
  270.1 6.0 %collective-permute-start.43 = (bf16[16,256]{1,0:T(8,128)(2,1)S(1)}, bf16[16,256]{1,0:T(8,128)(2,1)S(1)}, u32[]{:S(2)}, u32[]{:S(2)}) collective-permute-start(bf16[16,256]{1,0:T(8,128)(2,1)S(1)} %collective-permute-done.42), channel_id=1, source_target_pairs={{1,0},{2,1},{3,2},{4,3},{5,4},{6,5},{7,6},{8,7},{9,8},{10,9},{11,1... | collective-permute-start | bytes 24584 | tf_op jit(solution)/shard_map/ppermute | solution.py:27
  277.6 10.4 %gather_fusion.7 = bf16[3200,256]{1,0:T(8,128)(2,1)} fusion(bf16[3328,256]{1,0:T(8,128)(2,1)S(1)} %pad_maximum_fusion.2, s32[4096]{0:T(1024)} %copy-done.16), kind=kCustom, calls=%fused_computation.6.clone | custom fusion | bytes 3289600 | tf_op jit(solution)/shard_map/jit(_take)/gather | solution.py:142
  291.3 6.6 %collective-permute-start.47 = (bf16[3,1,64,256]{3,2,1,0:T(8,128)(2,1)}, bf16[3,1,64,256]{3,2,1,0:T(8,128)(2,1)}, u32[]{:S(2)}, u32[]{:S(2)}) collective-permute-start(bf16[3,1,64,256]{3,2,1,0:T(8,128)(2,1)} %pad_maximum_fusion.8), channel_id=1, source_target_pairs={{1,0},{2,1},{3,2},{4,3},{5,4},{6,5},{7,6},{8,7},{9,8},{10,9},{11,1... | collective-permute-start | bytes 294920 | tf_op jit(solution)/shard_map/ppermute | solution.py:19
  297.8 4.4 %fusion.5 = bf16[3200,256]{1,0:T(8,128)(2,1)S(1)} fusion(bf16[3200,256]{1,0:T(8,128)(2,1)S(1)} %reshape.202, bf16[3200,256]{1,0:T(8,128)(2,1)} %gather_fusion.7, pred[3200]{0:T(1024)(128)(4,1)S(1)} %compare_and_fusion.1, pred[3200]{0:T(1024)(128)(4,1)S(1)} %broadcast_in_dim.147), kind=kLoop, calls=%fused_computation.23 | loop fusion | flops 5734400 | bytes 4921600 | tf_op jit(solution)/shard_map/convert_element_type | solution.py:147
  306.0 10.3 %gather_fusion.8 = bf16[3200,512]{1,0:T(8,128)(2,1)} fusion(bf16[576,512]{1,0:T(8,128)(2,1)S(1)} %convolution_convert_fusion, s32[4096]{0:T(1024)S(1)} %copy-done.15), kind=kCustom, calls=%fused_computation.8.clone | custom fusion | bytes 6566400 | tf_op jit(solution)/shard_map/jit(_take)/gather | solution.py:140
  330.0 3.3 select_convert_fusion
  (286 shorter events, 151.8 us)
Async XLA Ops:
  0.6 75.1 %collective-permute-start.12 = (bf16[1,1,64,256]{3,2,1,0:T(8,128)(2,1)}, bf16[1,1,64,256]{3,2,1,0:T(8,128)(2,1)}, u32[]{:S(2)}, u32[]{:S(2)}) collective-permute-start(bf16[1,1,64,256]{3,2,1,0:T(8,128)(2,1)} %bitcast.186), channel_id=1, source_target_pairs={{0,16},{16,32},{32,48},{48,64},{64,80},{80,96},{96,112},{1,17},{17... | collective-permute-start | bytes 98312 | tf_op jit(solution)/shard_map/ppermute | solution.py:18
  2.7 73.1 %collective-permute-start.13 = (bf16[1,1,64,256]{3,2,1,0:T(8,128)(2,1)}, bf16[1,1,64,256]{3,2,1,0:T(8,128)(2,1)}, u32[]{:S(2)}, u32[]{:S(2)}) collective-permute-start(bf16[1,1,64,256]{3,2,1,0:T(8,128)(2,1)} %bitcast.187), channel_id=1, source_target_pairs={{16,0},{32,16},{48,32},{64,48},{80,64},{96,80},{112,96},{17,1},{33... | collective-permute-start | bytes 98312 | tf_op jit(solution)/shard_map/ppermute | solution.py:19
  15.2 12.9 %collective-permute-start = (bf16[16,256]{1,0:T(8,128)(2,1)S(1)}, bf16[16,256]{1,0:T(8,128)(2,1)S(1)}, u32[]{:S(2)}, u32[]{:S(2)}) collective-permute-start(bf16[16,256]{1,0:T(8,128)(2,1)S(1)} %get-tuple-element.40), channel_id=1, source_target_pairs={{0,16},{16,32},{32,48},{48,64},{64,80},{80,96},{96,112},{1,17},{17... | collective-permute-start | bytes 24584 | tf_op jit(solution)/shard_map/ppermute | solution.py:27
  17.1 20.7 %collective-permute-start.2 = (bf16[16,256]{1,0:T(8,128)(2,1)S(1)}, bf16[16,256]{1,0:T(8,128)(2,1)S(1)}, u32[]{:S(2)}, u32[]{:S(2)}) collective-permute-start(bf16[16,256]{1,0:T(8,128)(2,1)S(1)} %get-tuple-element.39), channel_id=1, source_target_pairs={{0,16},{16,32},{32,48},{48,64},{64,80},{80,96},{96,112},{1,17},{17... | collective-permute-start | bytes 24584 | tf_op jit(solution)/shard_map/ppermute | solution.py:27
  20.4 23.5 %collective-permute-start.3 = (bf16[16,256]{1,0:T(8,128)(2,1)S(1)}, bf16[16,256]{1,0:T(8,128)(2,1)S(1)}, u32[]{:S(2)}, u32[]{:S(2)}) collective-permute-start(bf16[16,256]{1,0:T(8,128)(2,1)S(1)} %get-tuple-element.38), channel_id=1, source_target_pairs={{0,16},{16,32},{32,48},{48,64},{64,80},{80,96},{96,112},{1,17},{17... | collective-permute-start | bytes 24584 | tf_op jit(solution)/shard_map/ppermute | solution.py:27
  35.9 15.5 %collective-permute-start.5 = (bf16[16,256]{1,0:T(8,128)(2,1)S(1)}, bf16[16,256]{1,0:T(8,128)(2,1)S(1)}, u32[]{:S(2)}, u32[]{:S(2)}) collective-permute-start(bf16[16,256]{1,0:T(8,128)(2,1)S(1)} %get-tuple-element.37), channel_id=1, source_target_pairs={{0,1},{1,2},{2,3},{3,4},{4,5},{5,6},{6,7},{7,8},{8,9},{9,10},{10,1... | collective-permute-start | bytes 24584 | tf_op jit(solution)/shard_map/ppermute | solution.py:27
  37.8 16.3 %collective-permute-start.6 = (bf16[16,256]{1,0:T(8,128)(2,1)S(1)}, bf16[16,256]{1,0:T(8,128)(2,1)S(1)}, u32[]{:S(2)}, u32[]{:S(2)}) collective-permute-start(bf16[16,256]{1,0:T(8,128)(2,1)S(1)} %get-tuple-element.36), channel_id=1, source_target_pairs={{1,0},{2,1},{3,2},{4,3},{5,4},{6,5},{7,6},{8,7},{9,8},{10,9},{11,1... | collective-permute-start | bytes 24584 | tf_op jit(solution)/shard_map/ppermute | solution.py:27
  54.1 10.0 %collective-permute-start.9 = (bf16[16,256]{1,0:T(8,128)(2,1)S(1)}, bf16[16,256]{1,0:T(8,128)(2,1)S(1)}, u32[]{:S(2)}, u32[]{:S(2)}) collective-permute-start(bf16[16,256]{1,0:T(8,128)(2,1)S(1)} %get-tuple-element.34), channel_id=1, source_target_pairs={{16,0},{32,16},{48,32},{64,48},{80,64},{96,80},{112,96},{17,1},{33... | collective-permute-start | bytes 24584 | tf_op jit(solution)/shard_map/ppermute | solution.py:27
  56.1 8.0 %collective-permute-start.8 = (bf16[16,256]{1,0:T(8,128)(2,1)S(1)}, bf16[16,256]{1,0:T(8,128)(2,1)S(1)}, u32[]{:S(2)}, u32[]{:S(2)}) collective-permute-start(bf16[16,256]{1,0:T(8,128)(2,1)S(1)} %collective-permute-done.7), channel_id=1, source_target_pairs={{0,1},{1,2},{2,3},{3,4},{4,5},{5,6},{6,7},{7,8},{8,9},{9,10},{10,1... | collective-permute-start | bytes 24584 | tf_op jit(solution)/shard_map/ppermute | solution.py:27
  77.2 14.3 %collective-permute-start.14 = (bf16[3,1,64,256]{3,2,1,0:T(8,128)(2,1)}, bf16[3,1,64,256]{3,2,1,0:T(8,128)(2,1)S(1)}, u32[]{:S(2)}, u32[]{:S(2)}) collective-permute-start(bf16[3,1,64,256]{3,2,1,0:T(8,128)(2,1)} %pad_maximum_fusion.6), channel_id=1, source_target_pairs={{0,1},{1,2},{2,3},{3,4},{4,5},{5,6},{6,7},{7,8},{8,9},{9,10},{10,1... | collective-permute-start | bytes 294920 | tf_op jit(solution)/shard_map/ppermute | solution.py:18
  79.1 12.4 %collective-permute-start.15 = (bf16[3,1,64,256]{3,2,1,0:T(8,128)(2,1)}, bf16[3,1,64,256]{3,2,1,0:T(8,128)(2,1)}, u32[]{:S(2)}, u32[]{:S(2)}) collective-permute-start(bf16[3,1,64,256]{3,2,1,0:T(8,128)(2,1)} %pad_maximum_fusion.6), channel_id=1, source_target_pairs={{1,0},{2,1},{3,2},{4,3},{5,4},{6,5},{7,6},{8,7},{9,8},{10,9},{11,1... | collective-permute-start | bytes 294920 | tf_op jit(solution)/shard_map/ppermute | solution.py:19
  127.9 53.9 %collective-permute-start.28 = (bf16[1,1,64,256]{3,2,1,0:T(8,128)(2,1)S(1)}, bf16[1,1,64,256]{3,2,1,0:T(8,128)(2,1)S(1)}, u32[]{:S(2)}, u32[]{:S(2)}) collective-permute-start(bf16[1,1,64,256]{3,2,1,0:T(8,128)(2,1)S(1)} %bitcast.178), channel_id=1, source_target_pairs={{0,16},{16,32},{32,48},{48,64},{64,80},{80,96},{96,112},{1,17},{17... | collective-permute-start | bytes 98312 | tf_op jit(solution)/shard_map/ppermute | solution.py:18
  131.2 50.6 %collective-permute-start.29 = (bf16[1,1,64,256]{3,2,1,0:T(8,128)(2,1)S(1)}, bf16[1,1,64,256]{3,2,1,0:T(8,128)(2,1)}, u32[]{:S(2)}, u32[]{:S(2)}) collective-permute-start(bf16[1,1,64,256]{3,2,1,0:T(8,128)(2,1)S(1)} %bitcast.179), channel_id=1, source_target_pairs={{16,0},{32,16},{48,32},{64,48},{80,64},{96,80},{112,96},{17,1},{33... | collective-permute-start | bytes 98312 | tf_op jit(solution)/shard_map/ppermute | solution.py:19
  133.5 8.3 %collective-permute-start.17 = (bf16[16,256]{1,0:T(8,128)(2,1)S(1)}, bf16[16,256]{1,0:T(8,128)(2,1)S(1)}, u32[]{:S(2)}, u32[]{:S(2)}) collective-permute-start(bf16[16,256]{1,0:T(8,128)(2,1)S(1)} %collective-permute-done.16), channel_id=1, source_target_pairs={{0,1},{1,2},{2,3},{3,4},{4,5},{5,6},{6,7},{7,8},{8,9},{9,10},{10,1... | collective-permute-start | bytes 24584 | tf_op jit(solution)/shard_map/ppermute | solution.py:27
  138.6 11.2 %collective-permute-start.19 = (bf16[16,256]{1,0:T(8,128)(2,1)S(1)}, bf16[16,256]{1,0:T(8,128)(2,1)S(1)}, u32[]{:S(2)}, u32[]{:S(2)}) collective-permute-start(bf16[16,256]{1,0:T(8,128)(2,1)S(1)} %get-tuple-element.30), channel_id=1, source_target_pairs={{0,16},{16,32},{32,48},{48,64},{64,80},{80,96},{96,112},{1,17},{17... | collective-permute-start | bytes 24584 | tf_op jit(solution)/shard_map/ppermute | solution.py:27
  141.8 15.5 %collective-permute-start.21 = (bf16[16,256]{1,0:T(8,128)(2,1)S(1)}, bf16[16,256]{1,0:T(8,128)(2,1)S(1)}, u32[]{:S(2)}, u32[]{:S(2)}) collective-permute-start(bf16[16,256]{1,0:T(8,128)(2,1)S(1)} %get-tuple-element.29), channel_id=1, source_target_pairs={{0,1},{1,2},{2,3},{3,4},{4,5},{5,6},{6,7},{7,8},{8,9},{9,10},{10,1... | collective-permute-start | bytes 24584 | tf_op jit(solution)/shard_map/ppermute | solution.py:27
  143.7 16.3 %collective-permute-start.22 = (bf16[16,256]{1,0:T(8,128)(2,1)S(1)}, bf16[16,256]{1,0:T(8,128)(2,1)S(1)}, u32[]{:S(2)}, u32[]{:S(2)}) collective-permute-start(bf16[16,256]{1,0:T(8,128)(2,1)S(1)} %get-tuple-element.28), channel_id=1, source_target_pairs={{1,0},{2,1},{3,2},{4,3},{5,4},{6,5},{7,6},{8,7},{9,8},{10,9},{11,1... | collective-permute-start | bytes 24584 | tf_op jit(solution)/shard_map/ppermute | solution.py:27
  160.1 10.0 %collective-permute-start.25 = (bf16[16,256]{1,0:T(8,128)(2,1)S(1)}, bf16[16,256]{1,0:T(8,128)(2,1)S(1)}, u32[]{:S(2)}, u32[]{:S(2)}) collective-permute-start(bf16[16,256]{1,0:T(8,128)(2,1)S(1)} %get-tuple-element.26), channel_id=1, source_target_pairs={{16,0},{32,16},{48,32},{64,48},{80,64},{96,80},{112,96},{17,1},{33... | collective-permute-start | bytes 24584 | tf_op jit(solution)/shard_map/ppermute | solution.py:27
  162.0 8.0 %collective-permute-start.24 = (bf16[16,256]{1,0:T(8,128)(2,1)S(1)}, bf16[16,256]{1,0:T(8,128)(2,1)S(1)}, u32[]{:S(2)}, u32[]{:S(2)}) collective-permute-start(bf16[16,256]{1,0:T(8,128)(2,1)S(1)} %collective-permute-done.23), channel_id=1, source_target_pairs={{0,1},{1,2},{2,3},{3,4},{4,5},{5,6},{6,7},{7,8},{8,9},{9,10},{10,1... | collective-permute-start | bytes 24584 | tf_op jit(solution)/shard_map/ppermute | solution.py:27
  183.2 14.4 %collective-permute-start.30 = (bf16[3,1,64,256]{3,2,1,0:T(8,128)(2,1)}, bf16[3,1,64,256]{3,2,1,0:T(8,128)(2,1)S(1)}, u32[]{:S(2)}, u32[]{:S(2)}) collective-permute-start(bf16[3,1,64,256]{3,2,1,0:T(8,128)(2,1)} %pad_maximum_fusion.7), channel_id=1, source_target_pairs={{0,1},{1,2},{2,3},{3,4},{4,5},{5,6},{6,7},{7,8},{8,9},{9,10},{10,1... | collective-permute-start | bytes 294920 | tf_op jit(solution)/shard_map/ppermute | solution.py:18
  185.2 12.5 %collective-permute-start.31 = (bf16[3,1,64,256]{3,2,1,0:T(8,128)(2,1)}, bf16[3,1,64,256]{3,2,1,0:T(8,128)(2,1)}, u32[]{:S(2)}, u32[]{:S(2)}) collective-permute-start(bf16[3,1,64,256]{3,2,1,0:T(8,128)(2,1)} %pad_maximum_fusion.7), channel_id=1, source_target_pairs={{1,0},{2,1},{3,2},{4,3},{5,4},{6,5},{7,6},{8,7},{9,8},{10,9},{11,1... | collective-permute-start | bytes 294920 | tf_op jit(solution)/shard_map/ppermute | solution.py:19
  231.7 7.9 %collective-permute-start.32 = (bf16[16,256]{1,0:T(8,128)(2,1)S(1)}, bf16[16,256]{1,0:T(8,128)(2,1)S(1)}, u32[]{:S(2)}, u32[]{:S(2)}) collective-permute-start(bf16[16,256]{1,0:T(8,128)(2,1)S(1)} %get-tuple-element.24), channel_id=1, source_target_pairs={{0,16},{16,32},{32,48},{48,64},{64,80},{80,96},{96,112},{1,17},{17... | collective-permute-start | bytes 24584 | tf_op jit(solution)/shard_map/ppermute | solution.py:27
  234.0 53.9 %collective-permute-start.44 = (bf16[1,1,64,256]{3,2,1,0:T(8,128)(2,1)S(1)}, bf16[1,1,64,256]{3,2,1,0:T(8,128)(2,1)S(1)}, u32[]{:S(2)}, u32[]{:S(2)}) collective-permute-start(bf16[1,1,64,256]{3,2,1,0:T(8,128)(2,1)S(1)} %bitcast.182), channel_id=1, source_target_pairs={{0,16},{16,32},{32,48},{48,64},{64,80},{80,96},{96,112},{1,17},{17... | collective-permute-start | bytes 98312 | tf_op jit(solution)/shard_map/ppermute | solution.py:18
  237.3 50.6 %collective-permute-start.45 = (bf16[1,1,64,256]{3,2,1,0:T(8,128)(2,1)S(1)}, bf16[1,1,64,256]{3,2,1,0:T(8,128)(2,1)}, u32[]{:S(2)}, u32[]{:S(2)}) collective-permute-start(bf16[1,1,64,256]{3,2,1,0:T(8,128)(2,1)S(1)} %bitcast.183), channel_id=1, source_target_pairs={{16,0},{32,16},{48,32},{64,48},{80,64},{96,80},{112,96},{17,1},{33... | collective-permute-start | bytes 98312 | tf_op jit(solution)/shard_map/ppermute | solution.py:19
  239.6 8.3 %collective-permute-start.33 = (bf16[16,256]{1,0:T(8,128)(2,1)S(1)}, bf16[16,256]{1,0:T(8,128)(2,1)S(1)}, u32[]{:S(2)}, u32[]{:S(2)}) collective-permute-start(bf16[16,256]{1,0:T(8,128)(2,1)S(1)} %collective-permute-done.32), channel_id=1, source_target_pairs={{0,1},{1,2},{2,3},{3,4},{4,5},{5,6},{6,7},{7,8},{8,9},{9,10},{10,1... | collective-permute-start | bytes 24584 | tf_op jit(solution)/shard_map/ppermute | solution.py:27
  244.7 11.2 %collective-permute-start.35 = (bf16[16,256]{1,0:T(8,128)(2,1)S(1)}, bf16[16,256]{1,0:T(8,128)(2,1)S(1)}, u32[]{:S(2)}, u32[]{:S(2)}) collective-permute-start(bf16[16,256]{1,0:T(8,128)(2,1)S(1)} %get-tuple-element.22), channel_id=1, source_target_pairs={{0,16},{16,32},{32,48},{48,64},{64,80},{80,96},{96,112},{1,17},{17... | collective-permute-start | bytes 24584 | tf_op jit(solution)/shard_map/ppermute | solution.py:27
  247.9 15.5 %collective-permute-start.37 = (bf16[16,256]{1,0:T(8,128)(2,1)S(1)}, bf16[16,256]{1,0:T(8,128)(2,1)S(1)}, u32[]{:S(2)}, u32[]{:S(2)}) collective-permute-start(bf16[16,256]{1,0:T(8,128)(2,1)S(1)} %get-tuple-element.21), channel_id=1, source_target_pairs={{0,1},{1,2},{2,3},{3,4},{4,5},{5,6},{6,7},{7,8},{8,9},{9,10},{10,1... | collective-permute-start | bytes 24584 | tf_op jit(solution)/shard_map/ppermute | solution.py:27
  249.9 16.3 %collective-permute-start.38 = (bf16[16,256]{1,0:T(8,128)(2,1)S(1)}, bf16[16,256]{1,0:T(8,128)(2,1)S(1)}, u32[]{:S(2)}, u32[]{:S(2)}) collective-permute-start(bf16[16,256]{1,0:T(8,128)(2,1)S(1)} %get-tuple-element.20), channel_id=1, source_target_pairs={{1,0},{2,1},{3,2},{4,3},{5,4},{6,5},{7,6},{8,7},{9,8},{10,9},{11,1... | collective-permute-start | bytes 24584 | tf_op jit(solution)/shard_map/ppermute | solution.py:27
  266.2 10.0 %collective-permute-start.41 = (bf16[16,256]{1,0:T(8,128)(2,1)S(1)}, bf16[16,256]{1,0:T(8,128)(2,1)S(1)}, u32[]{:S(2)}, u32[]{:S(2)}) collective-permute-start(bf16[16,256]{1,0:T(8,128)(2,1)S(1)} %get-tuple-element.18), channel_id=1, source_target_pairs={{16,0},{32,16},{48,32},{64,48},{80,64},{96,80},{112,96},{17,1},{33... | collective-permute-start | bytes 24584 | tf_op jit(solution)/shard_map/ppermute | solution.py:27
  268.1 8.0 %collective-permute-start.40 = (bf16[16,256]{1,0:T(8,128)(2,1)S(1)}, bf16[16,256]{1,0:T(8,128)(2,1)S(1)}, u32[]{:S(2)}, u32[]{:S(2)}) collective-permute-start(bf16[16,256]{1,0:T(8,128)(2,1)S(1)} %collective-permute-done.39), channel_id=1, source_target_pairs={{0,1},{1,2},{2,3},{3,4},{4,5},{5,6},{6,7},{7,8},{8,9},{9,10},{10,1... | collective-permute-start | bytes 24584 | tf_op jit(solution)/shard_map/ppermute | solution.py:27
  289.4 14.4 %collective-permute-start.46 = (bf16[3,1,64,256]{3,2,1,0:T(8,128)(2,1)}, bf16[3,1,64,256]{3,2,1,0:T(8,128)(2,1)S(1)}, u32[]{:S(2)}, u32[]{:S(2)}) collective-permute-start(bf16[3,1,64,256]{3,2,1,0:T(8,128)(2,1)} %pad_maximum_fusion.8), channel_id=1, source_target_pairs={{0,1},{1,2},{2,3},{3,4},{4,5},{5,6},{6,7},{7,8},{8,9},{9,10},{10,1... | collective-permute-start | bytes 294920 | tf_op jit(solution)/shard_map/ppermute | solution.py:18
  291.3 12.5 %collective-permute-start.47 = (bf16[3,1,64,256]{3,2,1,0:T(8,128)(2,1)}, bf16[3,1,64,256]{3,2,1,0:T(8,128)(2,1)}, u32[]{:S(2)}, u32[]{:S(2)}) collective-permute-start(bf16[3,1,64,256]{3,2,1,0:T(8,128)(2,1)} %pad_maximum_fusion.8), channel_id=1, source_target_pairs={{1,0},{2,1},{3,2},{4,3},{5,4},{6,5},{7,6},{8,7},{9,8},{10,9},{11,1... | collective-permute-start | bytes 294920 | tf_op jit(solution)/shard_map/ppermute | solution.py:19
  (59 other events, 588.3 us)
where the time goes:
time: 337 us; the launch traced here: 334 us
  starting transfers between devices  148 us (44%)
  local copies, waits for them, and re-layouts  101 us (30%)
  other arithmetic  48.8 us (14%)
  matrix products  18.3 us (5%)
  waiting for transfers between devices  14.5 us (4%)
    ppermute x36, starting transfers between devices, from_behind(): return lax.ppermute(block, axis, route)  106 us
    gather x3, local copies, waits for them, and re-layouts, on_device(): partner = jnp.take(lookup, partner_rows, axis=0)  31 us
    gather x3, local copies, waits for them, and re-layouts, on_device(): jnp.take(nbr_proj, source_rows, axis=0)  30.8 us
    ppermute x6, starting transfers between devices, extended(): after = lax.ppermute(first, axis, down)  27.8 us
    ppermute x36, waiting for transfers between devices, from_behind(): return lax.ppermute(block, axis, route)  14.5 us
    ppermute x6, starting transfers between devices, extended(): before = lax.ppermute(last, axis, up)  14.4 us
    convert_element_type x3, other arithmetic, on_device(): averaged = jnp.where(has_mirror, (edge_rows.astype(jnp.float32) + partner...  13.2 us
    select_n x4, other arithmetic, on_device(): jnp.take(nbr_proj, source_rows, axis=0)  9.2 us
  transfers between devices with their start and end apart: 48, of which 7 were waited for; matrix products, arithmetic and copies ran while one was open for 20% of the time, Pallas kernels for 0%

commit v1 on v0

v1 whole, which is shorter than its diff:
```python
import functools
import math

import jax
import jax.numpy as jnp
from jax import lax
from jax.experimental import pallas as pl
from jax.experimental.pallas import tpu as pltpu
from jax.sharding import PartitionSpec as P

LAYERS = 3
CITIES = 64
SLOTS = 50
WIDTH = 256
ROWS = CITIES * SLOTS
CAP = 16
INCOMING = 8 * CAP
LOOKUP = ROWS + INCOMING
EARLY = 3072
PICK = 768
CHUNK = 640
MESH = pl.DeviceIdType.MESH
F32 = jnp.float32
BF16 = jnp.bfloat16
OFFSETS = [(y, x) for y in (-1, 0, 1) for x in (-1, 0, 1) if (y, x) != (0, 0)]


def norm(values):
    centered = values - jnp.mean(values, axis=-1, keepdims=True)
    spread = jnp.mean(centered * centered, axis=-1, keepdims=True)
    return centered * lax.rsqrt(spread + 1e-05)


def split(values):
    high = values.astype(BF16).astype(F32)
    return high, values - high


def dot(a, b):
    return jnp.dot(a, b, preferred_element_type=F32)


def column(row, lanes):
    n = row.shape[1]
    eye = lax.broadcasted_iota(jnp.int32, (n, n), 0) == lanes
    return jnp.sum(jnp.where(eye, jnp.broadcast_to(row, (n, n)), 0.0), axis=1, keepdims=True)


def one_hot_tiles(index, value, tiles):
    n = index.shape[0]
    lanes = lax.broadcasted_iota(jnp.int32, (n, 128), 1)
    low = jnp.where(lanes == (index & 127), value, 0.0).astype(BF16)
    high = jnp.broadcast_to((index >> 7).astype(F32), (n, 128)).astype(BF16)
    zero = jnp.zeros((n, 128), BF16)
    return [jnp.where(high == jnp.asarray(t, BF16), low, zero) for t in range(tiles)]


def kernel(
    grid_y,
    grid_x,
    node_ref,
    edge_hbm,
    noisy_ref,
    nbr_ref,
    mirror_ref,
    send_ref,
    own_w,
    nbr_w,
    edge_w,
    noise_ref,
    emb_ref,
    time_embed,
    time_layer,
    node_out,
    edge_out,
    mix,
    pick,
    edges,
    averaged_early,
    picked_from,
    send_hot,
    fields,
    hist,
    nodes_in,
    edges_in,
    edges_sent,
    send_sem,
    recv_sem,
    copy_sem,
):
    here_y = lax.axis_index("ty")
    here_x = lax.axis_index("tx")
    targets = [
        (lax.rem(here_y - y + grid_y, grid_y), lax.rem(here_x - x + grid_x, grid_x))
        for y, x in OFFSETS
    ]
    barrier = pltpu.get_barrier_semaphore()
    for target in targets:
        pl.semaphore_signal(barrier, inc=1, device_id=target, device_id_type=MESH)

    load = pltpu.make_async_copy(edge_hbm, edges.at[0, pl.ds(0, ROWS)], copy_sem)
    load.start()

    def node_copy(layer, d, source):
        return pltpu.make_async_remote_copy(
            src_ref=source,
            dst_ref=nodes_in.at[layer, pl.ds(d * CITIES, CITIES)],
            send_sem=send_sem.at[layer, d],
            recv_sem=recv_sem.at[layer, d],
            device_id=targets[d],
            device_id_type=MESH,
        )

    def edge_copy(layer, d):
        return pltpu.make_async_remote_copy(
            src_ref=edges_sent.at[layer, pl.ds(d * CAP, CAP)],
            dst_ref=edges_in.at[layer, pl.ds(d * CAP, CAP)],
            send_sem=send_sem.at[layer, 8 + d],
            recv_sem=recv_sem.at[layer, 8 + d],
            device_id=targets[d],
            device_id_type=MESH,
        )

    nbr = nbr_ref[...]
    valid = nbr >= 0
    safe = jnp.maximum(nbr, 0)
    tile = safe >> 6
    rel = ((tile >> 4) - here_y + 1) * 3 + (tile & 15) - here_x + 1
    block = jnp.where(rel < 4, rel, jnp.where(rel == 4, 8, rel - 1))
    pick_at = jnp.where(valid, block * CITIES + (safe & 63), -1)
    mirror = mirror_ref[...]
    city = (mirror * 5243) >> 18
    local = (mirror - city * SLOTS) * CITIES + city
    came = (mirror - ROWS) >> 4
    came = came + jnp.where(came >= 4, 1, 0)
    came_y = (came * 11) >> 5
    from_y = here_y + came_y - 1
    from_x = here_x + (came - 3 * came_y) - 1
    inside = (from_y >= 0) & (from_y < grid_y) & (from_x >= 0) & (from_x < grid_x)
    remote = jnp.where(inside, mirror, -1)
    has = mirror >= 0
    partner_at = jnp.where(has, jnp.where(mirror >= ROWS, remote, local), -1)
    packed = (partner_at + 1) + jnp.where(has, 4096, 0) + (pick_at + 1) * 8192
    fields[...] = packed.astype(F32)

    hist[0] = node_ref[...]
    sends = send_ref[0]
    sent_city = (sends * 5243) >> 18
    sent_at = jnp.where(sends >= 0, (sends - sent_city * SLOTS) * CITIES + sent_city, -1)
    sent_at = sent_at.astype(F32)
    lanes16 = lax.broadcasted_iota(jnp.int32, (CAP, CAP), 1)
    for d in range(8):
        index = column(sent_at[d : d + 1], lanes16).astype(jnp.int32)
        for t, hot in enumerate(one_hot_tiles(index, 1.0, ROWS // 128)):
            send_hot[pl.ds(d * CAP, CAP), pl.ds(t * 128, 128)] = hot

    pl.semaphore_wait(barrier, 8)
    for d in range(8):
        node_copy(0, d, node_ref).start()
    load.wait()
    edges_sent[0] = dot(send_hot[...], edges[0, pl.ds(0, ROWS)]).astype(BF16)

    lanes64 = lax.broadcasted_iota(jnp.int32, (CITIES, CITIES), 1)
    lanes = lax.broadcasted_iota(jnp.int32, (CITIES, 128), 1)
    rows = lax.broadcasted_iota(jnp.int32, (CITIES, 128), 0)

    def build(k, carry):
        at = pl.ds(pl.multiple_of(k * CITIES, CITIES), CITIES)
        packed = column(fields[pl.ds(k, 1)], lanes64).astype(jnp.int32)
        noise = column(noisy_ref[pl.ds(k, 1)], lanes64)
        pick_at = (packed >> 13) - 1
        valid = pick_at >= 0
        has = ((packed >> 12) & 1) > 0
        partner_at = jnp.where(valid, (packed & 4095) - 1, -1)
        own_part = jnp.where(valid, jnp.where(has, 0.5, 1.0), 0.0)
        for t, hot in enumerate(one_hot_tiles(partner_at, 0.5, LOOKUP // 128)):
            mix[at, pl.ds(t * 128, 128)] = hot
        own_at = pl.ds(pl.multiple_of((k // 2) * 128, 128), 128)
        own = jnp.where(lanes == rows + lax.rem(k, 2) * CITIES, own_part, 0.0)
        mix[at, own_at] = (mix[at, own_at].astype(F32) + own).astype(BF16)
        hots = one_hot_tiles(pick_at, 1.0, 5)
        live = jnp.where(valid, 1.0, 0.0)
        for t in range(4):
            pick[at, pl.ds(t * 128, 128)] = hots[t]
        high = jnp.where(lanes == rows + CITIES, live, 0.0)
        pick[at, pl.ds(512, 128)] = (hots[4].astype(F32) + high).astype(BF16)
        noise_high, noise_low = split(noise * live)
        low = jnp.where(lanes == rows, live, 0.0)
        low = jnp.where((lanes == 64) | (lanes == 66), noise_high, low)
        low = jnp.where(lanes == 65, noise_low, low)
        pick[at, pl.ds(640, 128)] = low.astype(BF16)
        return carry

    lax.fori_loop(0, SLOTS, build, 0)
    for d in range(8):
        edge_copy(0, d).start()

    noise_high, noise_low = split(noise_ref[...])
    which = lax.broadcasted_iota(jnp.int32, (CITIES, WIDTH), 0)
    noise_rows = jnp.where(which < 2, noise_high, jnp.where(which == 2, noise_low, 0.0))
    picked_from[pl.ds(704, 64), pl.ds(0, WIDTH)] = noise_rows.astype(BF16)
    picked_from[pl.ds(576, 192), pl.ds(WIDTH, WIDTH)] = jnp.zeros((192, WIDTH), BF16)
    hidden = jnp.dot(
        emb_ref[...], time_embed[...], precision=lax.Precision.HIGHEST, preferred_element_type=F32
    )
    hidden = jnp.maximum(hidden, 0.0)

    def layer(l, carry):
        now = lax.rem(l, 2)
        later = 1 - now

        def early(ch, carry):
            at = pl.ds(pl.multiple_of(ch * CHUNK, CHUNK), CHUNK)
            averaged_early[at] = dot(mix[at, pl.ds(0, EARLY)], edges[now, pl.ds(0, EARLY)])
            return carry

        lax.fori_loop(0, ROWS // CHUNK, early, 0)
        nodes = hist[l]
        own = dot(nodes, own_w[l])
        time_row = jnp.dot(
            hidden, time_layer[l], precision=lax.Precision.HIGHEST, preferred_element_type=F32
        )
        high, low = split(own[:, :WIDTH] + time_row[0:1])
        picked_from[pl.ds(576, 64), pl.ds(0, WIDTH)] = high.astype(BF16)
        picked_from[pl.ds(640, 64), pl.ds(0, WIDTH)] = low.astype(BF16)
        picked_from[pl.ds(512, 64)] = dot(nodes, nbr_w[l]).astype(BF16)
        for d in range(8):
            node_copy(l, d, node_ref).wait_recv()
        picked_from[pl.ds(0, 512)] = dot(nodes_in[l], nbr_w[l]).astype(BF16)
        for d in range(8):
            edge_copy(l, d).wait_recv()
        edges[now, pl.ds(ROWS, INCOMING)] = edges_in[l]

        def late(ch, total):
            at = pl.ds(pl.multiple_of(ch * CHUNK, CHUNK), CHUNK)
            averaged = averaged_early[at] + dot(
                mix[at, pl.ds(EARLY, LOOKUP - EARLY)], edges[now, pl.ds(EARLY, LOOKUP - EARLY)]
            )
            averaged = averaged.astype(BF16)
            picked = dot(pick[at], picked_from[...])
            pre = picked[:, :WIDTH] + dot(averaged, edge_w[l])
            message = picked[:, WIDTH:]
            gated = message + jnp.tanh(0.5 * pre) * message
            total = total + jnp.sum(gated.reshape(CHUNK // CITIES, CITIES, WIDTH), axis=0)
            following = averaged.astype(F32) + jnp.maximum(norm(pre), 0.0)
            edges[later, at] = following.astype(BF16)
            return total

        total = lax.fori_loop(0, ROWS // CHUNK, late, jnp.zeros((CITIES, WIDTH), F32))
        update = jnp.maximum(norm(own[:, WIDTH:] + 0.5 * total), 0.0)
        hist[l + 1] = (nodes.astype(F32) + update).astype(BF16)

        @pl.when(l < LAYERS - 1)
        def _():
            edges_sent[l + 1] = dot(send_hot[...], edges[later, pl.ds(0, ROWS)]).astype(BF16)
            for d in range(8):
                node_copy(l + 1, d, hist.at[l + 1]).start()
            for d in range(8):
                edge_copy(l + 1, d).start()

        return carry

    lax.fori_loop(0, LAYERS, layer, 0)
    store = pltpu.make_async_copy(edges.at[LAYERS % 2, pl.ds(0, ROWS)], edge_out, copy_sem)
    store.start()
    node_out[...] = hist[LAYERS]

    def drain(l, carry):
        for d in range(8):
            node_copy(l, d, node_ref).wait_send()
            edge_copy(l, d).wait_send()
        return carry

    lax.fori_loop(0, LAYERS, drain, 0)
    store.wait()


def on_device(
    grid_y,
    grid_x,
    node_state,
    edge_state,
    noisy_edges,
    timestep,
    neighbors,
    mirror_src,
    send_rows,
    node_own,
    node_nbr,
    edge_weight,
    noise_embed,
    time_embed,
    time_layer,
):
    half = WIDTH // 2
    frequency = jnp.exp(-math.log(10000.0) * jnp.arange(half, dtype=F32) / half)
    phases = timestep[0].astype(F32) * frequency
    embedding = jnp.concatenate([jnp.cos(phases), jnp.sin(phases)])[None, :]
    embedding = jnp.broadcast_to(embedding, (8, WIDTH))
    edge_rows = jnp.transpose(edge_state, (1, 0, 2)).reshape(ROWS, WIDTH)
    vmem = pl.BlockSpec(memory_space=pltpu.VMEM)
    hbm = pl.BlockSpec(memory_space=pl.ANY)
    node_out, edge_out = pl.pallas_call(
        functools.partial(kernel, grid_y, grid_x),
        out_shape=(
            jax.ShapeDtypeStruct((CITIES, WIDTH), BF16),
            jax.ShapeDtypeStruct((ROWS, WIDTH), BF16),
        ),
        in_specs=[vmem, hbm] + [vmem] * 11,
        out_specs=(vmem, hbm),
        scratch_shapes=[
            pltpu.VMEM((ROWS, LOOKUP), BF16),
            pltpu.VMEM((ROWS, PICK), BF16),
            pltpu.VMEM((2, LOOKUP, WIDTH), BF16),
            pltpu.VMEM((ROWS, WIDTH), F32),
            pltpu.VMEM((PICK, 2 * WIDTH), BF16),
            pltpu.VMEM((INCOMING, ROWS), BF16),
            pltpu.VMEM((SLOTS, CITIES), F32),
            pltpu.VMEM((LAYERS + 1, CITIES, WIDTH), BF16),
            pltpu.VMEM((LAYERS, 8 * CITIES, WIDTH), BF16),
            pltpu.VMEM((LAYERS, INCOMING, WIDTH), BF16),
            pltpu.VMEM((LAYERS, INCOMING, WIDTH), BF16),
            pltpu.SemaphoreType.DMA((LAYERS, 16)),
            pltpu.SemaphoreType.DMA((LAYERS, 16)),
            pltpu.SemaphoreType.DMA,
        ],
        compiler_params=pltpu.CompilerParams(
            collective_id=0, has_side_effects=True, vmem_limit_bytes=60 * 1024 * 1024
        ),
    )(
        node_state,
        edge_rows,
        noisy_edges.T,
        neighbors.T,
        mirror_src.T,
        send_rows,
        node_own,
        node_nbr,
        edge_weight,
        noise_embed[None, :],
        embedding,
        time_embed,
        time_layer,
    )
    edge_out = edge_out.reshape(SLOTS, CITIES, WIDTH)
    return (node_out, jnp.transpose(edge_out, (1, 0, 2)))


def solution(mesh):
    rows = P(("ty", "tx"), None)
    cubes = P(("ty", "tx"), None, None)
    return jax.shard_map(
        functools.partial(on_device, mesh.shape["ty"], mesh.shape["tx"]),
        mesh=mesh,
        in_specs=(rows, cubes, rows, P(), rows, rows, cubes) + (P(),) * 6,
        out_specs=(rows, cubes),
        check_vma=False,
    )
```

time: 337 us -> 68.3 us (0.20)
  the two profiles are of different devices: /device:TPU:22 before, /device:TPU:1 now
where the time goes in v1:
time: 68.3 us; the launch traced here: 68.1 us
  Pallas kernels  62 us (91%)
  local copies, waits for them, and re-layouts  4.76 us (7%)
  between operations  1.3 us (2%)
    pallas_call x1, Pallas kernels, on_device(): pl.pallas_call(functools.partial(kernel, grid_y, grid_x), out_shape=(jax....  62 us
    unnamed x2, local copies, waits for them, and re-layouts  4.15 us

profile of v1, /device:TPU:1, one launch (start us, length us, event | category | flops | bytes accessed | tf_op | source)
XLA Modules:
  0.0 68.1 jit_solution(2789968240299740730)
XLA Ops:
  1.3 0.6 broadcast_in_dim.10.emb_ref
  1.9 62.0 %shard_map.140 = (bf16[64,256]{1,0:T(8,128)(2,1)}, bf16[3200,256]{1,0:T(8,128)(2,1)}) custom-call(bf16[64,256]{1,0:T(8,128)(2,1)} %node_ref.1, bf16[3200,256]{1,0:T(8,128)(2,1)} %bitcast.12, f32[50,64]{1,0:T(8,128)} %bitcast.13, s32[50,64]{1,0:T(8,128)} %bitcast.14, s32[50,64]{1,0:T(8,128)} %bitcast.15, s32[1,8,16]{2,1,0:T(8,128)} %send_ref.1, ...), custom_call_target="tpu_custom_call" | custom-call | tf_op jit(solution)/shard_map/pallas_call | solution.py:303
  63.9 1.4 %copy.18 = bf16[64,256]{1,0:T(8,128)(2,1)} copy(bf16[64,256]{1,0:T(8,128)(2,1)} %get-tuple-element.10) | data formatting | bytes 65536
  65.3 2.8 %copy.19 = bf16[64,50,256]{2,0,1:T(8,128)(2,1)} copy(bf16[64,50,256]{2,0,1:T(8,128)(2,1)} %bitcast.11) | data formatting | bytes 3276800
  (2 shorter events, 0.1 us)

commit v2 on v1

v2 whole, which is shorter than its diff:
```python
import functools
import math

import jax
import jax.numpy as jnp
from jax import lax
from jax.experimental import pallas as pl
from jax.experimental.pallas import tpu as pltpu
from jax.sharding import PartitionSpec as P

LAYERS = 3
CITIES = 64
SLOTS = 50
WIDTH = 256
HALF = 128
ROWS = CITIES * SLOTS
CAP = 16
INCOMING = 8 * CAP
PICK = 768
CHUNK = 640
CHUNKS = ROWS // CHUNK
GROUP = 2
MESH = pl.DeviceIdType.MESH
F32 = jnp.float32
BF16 = jnp.bfloat16
OFFSETS = [(y, x) for y in (-1, 0, 1) for x in (-1, 0, 1) if (y, x) != (0, 0)]


def norm(values):
    centered = values - jnp.mean(values, axis=-1, keepdims=True)
    spread = jnp.mean(centered * centered, axis=-1, keepdims=True)
    return centered * lax.rsqrt(spread + 1e-05)


def split(values):
    high = values.astype(BF16).astype(F32)
    return high, values - high


def dot(a, b):
    return jnp.dot(a, b, preferred_element_type=F32)


def exact_dot(a, b):
    return jnp.dot(a, b, precision=lax.Precision.HIGHEST, preferred_element_type=F32)


def column(row, eye):
    return jnp.sum(jnp.where(eye, jnp.broadcast_to(row, eye.shape), 0.0), axis=1, keepdims=True)


def halves(ref, start, count):
    left = ref[pl.ds(start * 2, count, stride=2), :]
    right = ref[pl.ds(start * 2 + 1, count, stride=2), :]
    return jnp.concatenate([left, right], axis=1)


def put_halves(ref, start, values):
    count = values.shape[0]
    ref[pl.ds(start * 2, count, stride=2), :] = values[:, :HALF]
    ref[pl.ds(start * 2 + 1, count, stride=2), :] = values[:, HALF:]


def kernel(
    grid_y,
    grid_x,
    node_ref,
    edge_hbm,
    noisy_ref,
    nbr_ref,
    mirror_ref,
    row_at,
    send_at,
    own_hbm,
    nbr_hbm,
    edge_w_hbm,
    noise_ref,
    emb_ref,
    time_embed_hbm,
    time_layer_hbm,
    node_out,
    edge_out,
    own_w,
    nbr_w,
    edge_w,
    time_embed,
    time_layer,
    raw,
    own_0,
    own_1,
    own_2,
    own_3,
    wide_0,
    wide_1,
    wide_2,
    gathered,
    pick,
    reach,
    picked_from,
    pre_buf,
    message_buf,
    averaged_buf,
    fields,
    sent_wide,
    time_rows,
    hist,
    nodes_in,
    edges_in,
    edges_sent,
    send_sem,
    recv_sem,
    copy_sem,
):
    owns = [own_0, own_1, own_2, own_3]
    wides = [wide_0, wide_1, wide_2]
    here_y = lax.axis_index("ty")
    here_x = lax.axis_index("tx")
    targets = [
        (lax.rem(here_y - y + grid_y, grid_y), lax.rem(here_x - x + grid_x, grid_x))
        for y, x in OFFSETS
    ]
    barrier = pltpu.get_barrier_semaphore()
    for target in targets:
        pl.semaphore_signal(barrier, inc=1, device_id=target, device_id_type=MESH)

    pairs = [
        (edge_hbm, raw),
        (time_embed_hbm, time_embed),
        (time_layer_hbm, time_layer),
        (own_hbm, own_w),
        (nbr_hbm, nbr_w),
        (edge_w_hbm, edge_w),
    ]
    loads = [pltpu.make_async_copy(s, t, copy_sem.at[i]) for i, (s, t) in enumerate(pairs)]
    for load in loads:
        load.start()

    def node_copy(layer, d, source):
        return pltpu.make_async_remote_copy(
            src_ref=source,
            dst_ref=nodes_in.at[layer, pl.ds(d * CITIES, CITIES)],
            send_sem=send_sem.at[layer, d],
            recv_sem=recv_sem.at[layer, d],
            device_id=targets[d],
            device_id_type=MESH,
        )

    def edge_copy(layer, d):
        return pltpu.make_async_remote_copy(
            src_ref=edges_sent.at[layer, pl.ds(d * CAP, CAP)],
            dst_ref=edges_in.at[layer, pl.ds(d * CAP, CAP)],
            send_sem=send_sem.at[layer, 8 + d],
            recv_sem=recv_sem.at[layer, 8 + d],
            device_id=targets[d],
            device_id_type=MESH,
        )

    nbr = nbr_ref[...]
    valid = nbr >= 0
    safe = jnp.maximum(nbr, 0)
    tile = safe >> 6
    rel = ((tile >> 4) - here_y + 1) * 3 + (tile & 15) - here_x + 1
    block = jnp.where(rel < 4, rel, jnp.where(rel == 4, 8, rel - 1))
    pick_at = jnp.where(valid, block * CITIES + (safe & 63), -1)
    mirror = mirror_ref[...]
    came = (mirror - ROWS) >> 4
    came = came + jnp.where(came >= 4, 1, 0)
    came_y = (came * 11) >> 5
    from_y = here_y + came_y - 1
    from_x = here_x + (came - 3 * came_y) - 1
    inside = (from_y >= 0) & (from_y < grid_y) & (from_x >= 0) & (from_x < grid_x)
    is_far = mirror >= ROWS
    far_at = jnp.where(valid & is_far & inside, mirror - ROWS, -1)
    fields[...] = ((far_at + 1) + (pick_at + 1) * 256).astype(F32)
    hist[0] = node_ref[...]
    for wide in wides:
        wide[pl.ds(2 * ROWS, 8)] = jnp.zeros((8, HALF), F32)
    noise_high, noise_low = split(noise_ref[...])
    which = lax.broadcasted_iota(jnp.int32, (CITIES, WIDTH), 0)
    noise_rows = jnp.where(which < 2, noise_high, jnp.where(which == 2, noise_low, 0.0))
    picked_from[pl.ds(704, 64), pl.ds(0, WIDTH)] = noise_rows.astype(BF16)
    picked_from[pl.ds(576, 192), pl.ds(WIDTH, WIDTH)] = jnp.zeros((192, WIDTH), BF16)

    loads[0].wait()

    def widen(ch, carry):
        at = pl.multiple_of(ch * CHUNK, CHUNK)
        put_halves(wide_0, at, raw[pl.ds(at, CHUNK)].astype(F32))
        return carry

    lax.fori_loop(0, CHUNKS, widen, 0)

    def send_edges(l):
        for d in range(8):
            for p in range(CAP):
                at = send_at[d, p]
                to = (d * CAP + p) * 2
                sent_wide[pl.ds(to, 1), :] = wides[l][pl.ds(at, 1), :]
                sent_wide[pl.ds(to + 1, 1), :] = wides[l][pl.ds(at + 1, 1), :]
        edges_sent[l] = halves(sent_wide, 0, INCOMING).astype(BF16)
        for d in range(8):
            edge_copy(l, d).start()

    pl.semaphore_wait(barrier, 8)
    for d in range(8):
        node_copy(0, d, node_ref).start()
    send_edges(0)

    def gather_slot(l, k):
        for c in range(CITIES):
            at = row_at[k, c]
            to = (k * CITIES + c) * 2
            gathered[pl.ds(to, 1), :] = wides[l][pl.ds(at, 1), :]
            gathered[pl.ds(to + 1, 1), :] = wides[l][pl.ds(at + 1, 1), :]

    eye = lax.broadcasted_iota(jnp.int32, (CITIES, CITIES), 1)
    eye = eye == lax.broadcasted_iota(jnp.int32, (CITIES, CITIES), 0)
    lanes = lax.broadcasted_iota(jnp.int32, (CITIES, HALF), 1)
    rows = lax.broadcasted_iota(jnp.int32, (CITIES, HALF), 0)
    zero = jnp.zeros((CITIES, HALF), BF16)

    def build(k, carry):
        at = pl.ds(pl.multiple_of(k * CITIES, CITIES), CITIES)
        packed = column(fields[pl.ds(k, 1)], eye).astype(jnp.int32)
        noise = column(noisy_ref[pl.ds(k, 1)], eye)
        packed = jnp.broadcast_to(packed, (CITIES, HALF))
        pick_at = (packed >> 8) - 1
        far_at = (packed & 255) - 1
        live = jnp.where(pick_at >= 0, 1.0, 0.0)
        reach[at] = jnp.where(lanes == far_at, 1.0, 0.0).astype(BF16)
        low = jnp.where(lanes == (pick_at & 127), 1.0, 0.0).astype(BF16)
        high = (pick_at >> 7).astype(F32).astype(BF16)
        hots = [jnp.where(high == jnp.asarray(t, BF16), low, zero) for t in range(5)]
        for t in range(4):
            pick[at, pl.ds(t * HALF, HALF)] = hots[t]
        own = jnp.where(lanes == rows + CITIES, live, 0.0)
        pick[at, pl.ds(512, HALF)] = hots[4] + own.astype(BF16)
        noise_high, noise_low = split(noise * live)
        rest = jnp.where(lanes == rows, live, 0.0)
        rest = jnp.where((lanes == 64) | (lanes == 66), noise_high, rest)
        rest = jnp.where(lanes == 65, noise_low, rest)
        pick[at, pl.ds(640, HALF)] = rest.astype(BF16)
        live = live.astype(BF16)
        own_0[at, pl.ds(0, HALF)] = raw[at, pl.ds(0, HALF)] * live
        own_0[at, pl.ds(HALF, HALF)] = raw[at, pl.ds(HALF, HALF)] * live
        gather_slot(0, k)
        return carry

    lax.fori_loop(0, SLOTS, build, 0)

    for load in loads[1:]:
        load.wait()
    hidden = jnp.maximum(exact_dot(emb_ref[...], time_embed[...]), 0.0)
    for l in range(LAYERS):
        time_rows[pl.ds(8 * l, 8)] = exact_dot(hidden, time_layer[l])

    for l in range(LAYERS):
        if l > 0:

            def gather(g, carry, l=l):
                for step in range(GROUP):
                    gather_slot(l, g * GROUP + step)
                return carry

            lax.fori_loop(0, SLOTS // GROUP, gather, 0)
        nodes = hist[l]
        own = dot(nodes, own_w[l])
        high, low = split(own[:, :WIDTH] + time_rows[pl.ds(8 * l, 1)])
        picked_from[pl.ds(576, 64), pl.ds(0, WIDTH)] = high.astype(BF16)
        picked_from[pl.ds(640, 64), pl.ds(0, WIDTH)] = low.astype(BF16)
        picked_from[pl.ds(512, 64)] = dot(nodes, nbr_w[l]).astype(BF16)
        for d in range(8):
            node_copy(l, d, node_ref).wait_recv()
        picked_from[pl.ds(0, 512)] = dot(nodes_in[l], nbr_w[l]).astype(BF16)
        for d in range(8):
            edge_copy(l, d).wait_recv()

        def multiply(ch, l=l):
            start = pl.multiple_of(ch * CHUNK, CHUNK)
            at = pl.ds(start, CHUNK)
            partner = halves(gathered, start, CHUNK) + dot(reach[at], edges_in[l])
            averaged = ((owns[l][at].astype(F32) + partner) * 0.5).astype(BF16)
            picked = dot(pick[at], picked_from[...])
            averaged_buf[...] = averaged
            pre_buf[...] = picked[:, :WIDTH] + dot(averaged, edge_w[l])
            message_buf[...] = picked[:, WIDTH:].astype(BF16)

        def apply(ch, total, l=l):
            start = pl.multiple_of(ch * CHUNK, CHUNK)
            pre = pre_buf[...]
            message = message_buf[...].astype(F32)
            gated = message + jnp.tanh(0.5 * pre) * message
            total = total + jnp.sum(gated.reshape(CHUNK // CITIES, CITIES, WIDTH), axis=0)
            following = averaged_buf[...].astype(F32) + jnp.maximum(norm(pre), 0.0)
            following = following.astype(BF16)
            owns[l + 1][pl.ds(start, CHUNK)] = following
            if l + 1 < LAYERS:
                put_halves(wides[l + 1], start, following.astype(F32))
            return total

        def both(ch, total):
            total = apply(ch - 1, total)
            multiply(ch)
            return total

        multiply(0)
        total = lax.fori_loop(1, CHUNKS, both, jnp.zeros((CITIES, WIDTH), F32))
        total = apply(CHUNKS - 1, total)
        update = jnp.maximum(norm(own[:, WIDTH:] + 0.5 * total), 0.0)
        hist[l + 1] = (nodes.astype(F32) + update).astype(BF16)
        if l + 1 < LAYERS:
            send_edges(l + 1)
            for d in range(8):
                node_copy(l + 1, d, hist.at[l + 1]).start()

    store = pltpu.make_async_copy(own_3, edge_out, copy_sem.at[0])
    store.start()
    node_out[...] = hist[LAYERS]

    def drain(l, carry):
        for d in range(8):
            node_copy(l, d, node_ref).wait_send()
            edge_copy(l, d).wait_send()
        return carry

    lax.fori_loop(0, LAYERS, drain, 0)
    store.wait()


def by_slot(row):
    city = row // SLOTS
    return (row - city * SLOTS) * CITIES + city


def on_device(
    grid_y,
    grid_x,
    node_state,
    edge_state,
    noisy_edges,
    timestep,
    neighbors,
    mirror_src,
    send_rows,
    node_own,
    node_nbr,
    edge_weight,
    noise_embed,
    time_embed,
    time_layer,
):
    half = WIDTH // 2
    frequency = jnp.exp(-math.log(10000.0) * jnp.arange(half, dtype=F32) / half)
    phases = timestep[0].astype(F32) * frequency
    embedding = jnp.concatenate([jnp.cos(phases), jnp.sin(phases)])[None, :]
    embedding = jnp.broadcast_to(embedding, (8, WIDTH))
    edge_rows = jnp.transpose(edge_state, (1, 0, 2)).reshape(ROWS, WIDTH)
    vmem = pl.BlockSpec(memory_space=pltpu.VMEM)
    hbm = pl.BlockSpec(memory_space=pl.ANY)
    smem = pl.BlockSpec(memory_space=pltpu.SMEM)
    nbr, mirror = neighbors.T, mirror_src.T
    itself = jnp.arange(ROWS, dtype=jnp.int32).reshape(SLOTS, CITIES)
    partner_at = jnp.where(mirror >= 0, jnp.where(mirror >= ROWS, ROWS, by_slot(mirror)), itself)
    row_at = jnp.where(nbr >= 0, partner_at, ROWS) * 2
    send_at = jnp.where(send_rows[0] >= 0, by_slot(send_rows[0]), ROWS) * 2
    node_out, edge_out = pl.pallas_call(
        functools.partial(kernel, grid_y, grid_x),
        out_shape=(
            jax.ShapeDtypeStruct((CITIES, WIDTH), BF16),
            jax.ShapeDtypeStruct((ROWS, WIDTH), BF16),
        ),
        in_specs=[vmem, hbm] + [vmem] * 3 + [smem] * 2 + [hbm] * 3 + [vmem] * 2 + [hbm] * 2,
        out_specs=(vmem, hbm),
        scratch_shapes=[
            pltpu.VMEM((LAYERS, WIDTH, 2 * WIDTH), BF16),
            pltpu.VMEM((LAYERS, WIDTH, 2 * WIDTH), BF16),
            pltpu.VMEM((LAYERS, WIDTH, WIDTH), BF16),
            pltpu.VMEM((WIDTH, WIDTH), F32),
            pltpu.VMEM((LAYERS, WIDTH, WIDTH), F32),
            pltpu.VMEM((ROWS, WIDTH), BF16),
        ]
        + [pltpu.VMEM((ROWS, WIDTH), BF16)] * 4
        + [pltpu.VMEM((2 * ROWS + 8, HALF), F32)] * 3
        + [
            pltpu.VMEM((2 * ROWS, HALF), F32),
            pltpu.VMEM((ROWS, PICK), BF16),
            pltpu.VMEM((ROWS, INCOMING), BF16),
            pltpu.VMEM((PICK, 2 * WIDTH), BF16),
            pltpu.VMEM((CHUNK, WIDTH), F32),
            pltpu.VMEM((CHUNK, WIDTH), BF16),
            pltpu.VMEM((CHUNK, WIDTH), BF16),
            pltpu.VMEM((SLOTS, CITIES), F32),
            pltpu.VMEM((2 * INCOMING, HALF), F32),
            pltpu.VMEM((8 * LAYERS, WIDTH), F32),
            pltpu.VMEM((LAYERS + 1, CITIES, WIDTH), BF16),
            pltpu.VMEM((LAYERS, 8 * CITIES, WIDTH), BF16),
            pltpu.VMEM((LAYERS, INCOMING, WIDTH), BF16),
            pltpu.VMEM((LAYERS, INCOMING, WIDTH), BF16),
            pltpu.SemaphoreType.DMA((LAYERS, 16)),
            pltpu.SemaphoreType.DMA((LAYERS, 16)),
            pltpu.SemaphoreType.DMA((8,)),
        ],
        compiler_params=pltpu.CompilerParams(
            collective_id=0, has_side_effects=True, vmem_limit_bytes=44 * 1024 * 1024
        ),
    )(
        node_state,
        edge_rows,
        noisy_edges.T,
        nbr,
        mirror,
        row_at,
        send_at,
        node_own,
        node_nbr,
        edge_weight,
        noise_embed[None, :],
        embedding,
        time_embed,
        time_layer,
    )
    edge_out = edge_out.reshape(SLOTS, CITIES, WIDTH)
    return (node_out, jnp.transpose(edge_out, (1, 0, 2)))


def solution(mesh):
    rows = P(("ty", "tx"), None)
    cubes = P(("ty", "tx"), None, None)
    return jax.shard_map(
        functools.partial(on_device, mesh.shape["ty"], mesh.shape["tx"]),
        mesh=mesh,
        in_specs=(rows, cubes, rows, P(), rows, rows, cubes) + (P(),) * 6,
        out_specs=(rows, cubes),
        check_vma=False,
    )
```

time: 68.3 us -> 64 us (0.937)
  Pallas kernels: 62 us -> 48.2 us
  local copies, waits for them, and re-layouts: 4.76 us -> 12.2 us
  other arithmetic: 0.06 us -> 1.57 us
    pallas_call x1, Pallas kernels: 62 us -> 48.2 us  [on_device(): pl.pallas_call(functools.partial(kernel, grid_y, grid_x), out_shape=(jax....]
    unnamed x2 -> x24, local copies, waits for them, and re-layouts: 4.15 us -> 12.2 us
    mul x0 -> x2, other arithmetic: none -> 1.51 us  [the longest x1 0.81 us: on_device(): row_at = jnp.where(nbr >= 0, partner_at, ROWS) * 2]
where the time goes in v2:
time: 64 us; the launch traced here: 63.3 us
  Pallas kernels  48.2 us (75%)
  local copies, waits for them, and re-layouts  12.2 us (19%)
  other arithmetic  1.57 us (2%)
  between operations  1.32 us (2%)
    pallas_call x1, Pallas kernels, on_device(): pl.pallas_call(functools.partial(kernel, grid_y, grid_x), out_shape=(jax....  48.2 us
    unnamed x24, local copies, waits for them, and re-layouts  12.2 us

profile of v2, /device:TPU:1, one launch (start us, length us, event | category | flops | bytes accessed | tf_op | source)
XLA Modules:
  0.0 63.3 jit_solution(1198507992582945973)
XLA Ops:
  1.3 0.7 %fusion.6.send_at = s32[8,16]{1,0:T(8,128)S(1)} fusion(s32[1,8,16]{2,1,0:T(8,128)} %param.19), kind=kLoop, calls=%fused_computation.16 | loop fusion | flops 1920 | bytes 1024 | tf_op jit(solution)/shard_map/mul | solution.py:365
  2.1 0.8 %select_multiply_fusion.row_at = s32[50,64]{1,0:T(8,128)S(1)} fusion(s32[64,50]{0,1:T(8,128)} %param.18, s32[64,50]{0,1:T(8,128)} %param.17), kind=kLoop, calls=%fused_computation.1 | loop fusion | flops 67200 | bytes 38400 | tf_op jit(solution)/shard_map/mul | solution.py:364
  2.9 0.0 copy-start
  2.9 1.4 %copy-done = bf16[64,50,256]{2,0,1:T(8,128)(2,1)S(1)} copy-done((bf16[64,50,256]{2,0,1:T(8,128)(2,1)S(1)}, bf16[64,50,256]{2,0,1:T(8,128)(2,1)}, u32[]{:S(2)}) %copy-start) | copy-done | bytes 1638424
  4.3 0.0 copy-start.1
  4.3 1.1 %copy-done.1 = bf16[3,256,512]{2,1,0:T(8,128)(2,1)S(1)} copy-done((bf16[3,256,512]{2,1,0:T(8,128)(2,1)S(1)}, bf16[3,256,512]{2,1,0:T(8,128)(2,1)}, u32[]{:S(2)}) %copy-start.1) | copy-done | bytes 786456
  5.4 0.0 copy-start.2
  5.4 1.1 %copy-done.2 = bf16[3,256,512]{2,1,0:T(8,128)(2,1)S(1)} copy-done((bf16[3,256,512]{2,1,0:T(8,128)(2,1)S(1)}, bf16[3,256,512]{2,1,0:T(8,128)(2,1)}, u32[]{:S(2)}) %copy-start.2) | copy-done | bytes 786456
  6.6 0.0 copy-start.3
  6.6 1.1 %copy-done.3 = f32[3,256,256]{2,1,0:T(8,128)S(1)} copy-done((f32[3,256,256]{2,1,0:T(8,128)S(1)}, f32[3,256,256]{2,1,0:T(8,128)}, u32[]{:S(2)}) %copy-start.3) | copy-done | bytes 786456
  7.7 0.0 copy-start.4
  7.7 1.0 %copy-done.4 = bf16[3,256,256]{2,1,0:T(8,128)(2,1)S(1)} copy-done((bf16[3,256,256]{2,1,0:T(8,128)(2,1)S(1)}, bf16[3,256,256]{2,1,0:T(8,128)(2,1)}, u32[]{:S(2)}) %copy-start.4) | copy-done | bytes 393240
  8.7 0.0 copy-start.5
  8.7 0.9 %copy-done.5 = f32[256,256]{1,0:T(8,128)S(1)} copy-done((f32[256,256]{1,0:T(8,128)S(1)}, f32[256,256]{1,0:T(8,128)}, u32[]{:S(2)}) %copy-start.5) | copy-done | bytes 262168
  9.6 0.0 copy-start.6
  9.7 0.7 %copy-done.6 = s32[64,50]{0,1:T(8,128)S(1)} copy-done((s32[64,50]{0,1:T(8,128)S(1)}, s32[64,50]{0,1:T(8,128)}, u32[]{:S(2)}) %copy-start.6) | copy-done | bytes 12824
  10.4 0.0 copy-start.7
  10.4 0.7 %copy-done.7 = s32[64,50]{0,1:T(8,128)S(1)} copy-done((s32[64,50]{0,1:T(8,128)S(1)}, s32[64,50]{0,1:T(8,128)}, u32[]{:S(2)}) %copy-start.7) | copy-done | bytes 12824
  11.1 0.0 copy-start.8
  11.1 0.8 %copy-done.8 = bf16[64,256]{1,0:T(8,128)(2,1)S(1)} copy-done((bf16[64,256]{1,0:T(8,128)(2,1)S(1)}, bf16[64,256]{1,0:T(8,128)(2,1)}, u32[]{:S(2)}) %copy-start.8) | copy-done | bytes 32792
  11.9 0.0 copy-start.9
  11.9 0.7 %copy-done.9 = f32[64,50]{0,1:T(8,128)S(1)} copy-done((f32[64,50]{0,1:T(8,128)S(1)}, f32[64,50]{0,1:T(8,128)}, u32[]{:S(2)}) %copy-start.9) | copy-done | bytes 12824
  12.7 0.0 copy-start.10
  12.7 0.7 %copy-done.10 = f32[256]{0:T(256)S(1)} copy-done((f32[256]{0:T(256)S(1)}, f32[256]{0:T(256)}, u32[]{:S(2)}) %copy-start.10) | copy-done | bytes 1048
  13.3 48.2 %shard_map.140 = (bf16[64,256]{1,0:T(8,128)(2,1)S(1)}, bf16[3200,256]{1,0:T(8,128)(2,1)S(1)}) custom-call(bf16[64,256]{1,0:T(8,128)(2,1)S(1)} %copy-done.8, bf16[3200,256]{1,0:T(8,128)(2,1)S(1)} %bitcast.43, f32[50,64]{1,0:T(8,128)S(1)} %bitcast.47, s32[50,64]{1,0:T(8,128)S(1)} %bitcast.45, s32[50,64]{1,0:T(8,128)S(1)} %bitcast.46, ...), custom_call_target="tpu_custom_call" | custom-call | tf_op jit(solution)/shard_map/pallas_call | solution.py:366
  61.5 0.6 copy.18
  62.1 1.2 %copy.19 = bf16[64,50,256]{2,0,1:T(8,128)(2,1)} copy(bf16[64,50,256]{2,0,1:T(8,128)(2,1)S(1)} %bitcast.44) | data formatting | bytes 3276800
  (3 shorter events, 0.1 us)
Async XLA Ops:
  2.9 1.4 %copy-start = (bf16[64,50,256]{2,0,1:T(8,128)(2,1)S(1)}, bf16[64,50,256]{2,0,1:T(8,128)(2,1)}, u32[]{:S(2)}) copy-start(bf16[64,50,256]{2,0,1:T(8,128)(2,1)} %param.14) | copy-start | bytes 4915204
  4.3 1.1 %copy-start.1 = (bf16[3,256,512]{2,1,0:T(8,128)(2,1)S(1)}, bf16[3,256,512]{2,1,0:T(8,128)(2,1)}, u32[]{:S(2)}) copy-start(bf16[3,256,512]{2,1,0:T(8,128)(2,1)} %own_hbm.1) | copy-start | bytes 2359300
  5.4 1.1 %copy-start.2 = (bf16[3,256,512]{2,1,0:T(8,128)(2,1)S(1)}, bf16[3,256,512]{2,1,0:T(8,128)(2,1)}, u32[]{:S(2)}) copy-start(bf16[3,256,512]{2,1,0:T(8,128)(2,1)} %nbr_hbm.1) | copy-start | bytes 2359300
  6.6 1.1 %copy-start.3 = (f32[3,256,256]{2,1,0:T(8,128)S(1)}, f32[3,256,256]{2,1,0:T(8,128)}, u32[]{:S(2)}) copy-start(f32[3,256,256]{2,1,0:T(8,128)} %time_layer_hbm.1) | copy-start | bytes 2359300
  7.7 1.0 %copy-start.4 = (bf16[3,256,256]{2,1,0:T(8,128)(2,1)S(1)}, bf16[3,256,256]{2,1,0:T(8,128)(2,1)}, u32[]{:S(2)}) copy-start(bf16[3,256,256]{2,1,0:T(8,128)(2,1)} %edge_w_hbm.1) | copy-start | bytes 1179652
  8.7 0.9 %copy-start.5 = (f32[256,256]{1,0:T(8,128)S(1)}, f32[256,256]{1,0:T(8,128)}, u32[]{:S(2)}) copy-start(f32[256,256]{1,0:T(8,128)} %time_embed_hbm.1) | copy-start | bytes 786436
  9.6 0.7 %copy-start.6 = (s32[64,50]{0,1:T(8,128)S(1)}, s32[64,50]{0,1:T(8,128)}, u32[]{:S(2)}) copy-start(s32[64,50]{0,1:T(8,128)} %param.17) | copy-start | bytes 38404
  10.4 0.7 %copy-start.7 = (s32[64,50]{0,1:T(8,128)S(1)}, s32[64,50]{0,1:T(8,128)}, u32[]{:S(2)}) copy-start(s32[64,50]{0,1:T(8,128)} %param.18) | copy-start | bytes 38404
  11.1 0.8 %copy-start.8 = (bf16[64,256]{1,0:T(8,128)(2,1)S(1)}, bf16[64,256]{1,0:T(8,128)(2,1)}, u32[]{:S(2)}) copy-start(bf16[64,256]{1,0:T(8,128)(2,1)} %node_ref.1) | copy-start | bytes 98308
  11.9 0.7 %copy-start.9 = (f32[64,50]{0,1:T(8,128)S(1)}, f32[64,50]{0,1:T(8,128)}, u32[]{:S(2)}) copy-start(f32[64,50]{0,1:T(8,128)} %param.15) | copy-start | bytes 38404
  12.7 0.7 %copy-start.10 = (f32[256]{0:T(256)S(1)}, f32[256]{0:T(256)}, u32[]{:S(2)}) copy-start(f32[256]{0:T(256)} %param.23) | copy-start | bytes 3076

commit v3 on v2

--- a/solution.py
+++ b/solution.py
@@ -20,16 +20,18 @@
 CHUNK = 640
 CHUNKS = ROWS // CHUNK
 GROUP = 2
+AHEAD = 2
+LATE = 1600
 MESH = pl.DeviceIdType.MESH
 F32 = jnp.float32
 BF16 = jnp.bfloat16
 OFFSETS = [(y, x) for y in (-1, 0, 1) for x in (-1, 0, 1) if (y, x) != (0, 0)]
 
 
-def norm(values):
+def norm(values, epsilon=1e-05):
     centered = values - jnp.mean(values, axis=-1, keepdims=True)
     spread = jnp.mean(centered * centered, axis=-1, keepdims=True)
-    return centered * lax.rsqrt(spread + 1e-05)
+    return centered * lax.rsqrt(spread + epsilon)
 
 
 def split(values):
@@ -64,22 +66,27 @@
 def kernel(
     grid_y,
     grid_x,
-    node_ref,
+    node_hbm,
     edge_hbm,
-    noisy_ref,
-    nbr_ref,
-    mirror_ref,
+    noisy_hbm,
+    nbr_ids_hbm,
+    mirror_hbm,
     row_at,
     send_at,
     own_hbm,
     nbr_hbm,
     edge_w_hbm,
-    noise_ref,
+    noise_hbm,
     emb_ref,
     time_embed_hbm,
     time_layer_hbm,
     node_out,
     edge_out,
+    node_ref,
+    noisy_ref,
+    nbr_ref,
+    mirror_ref,
+    noise_ref,
     own_w,
     nbr_w,
     edge_w,
@@ -87,8 +94,6 @@
     time_layer,
     raw,
     own_0,
-    own_1,
-    own_2,
     own_3,
     wide_0,
     wide_1,
@@ -97,9 +102,8 @@
     pick,
     reach,
     picked_from,
-    pre_buf,
-    message_buf,
-    averaged_buf,
+    pre_part,
+    messages,
     fields,
     sent_wide,
     time_rows,
@@ -111,7 +115,6 @@
     recv_sem,
     copy_sem,
 ):
-    owns = [own_0, own_1, own_2, own_3]
     wides = [wide_0, wide_1, wide_2]
     here_y = lax.axis_index("ty")
     here_x = lax.axis_index("tx")
@@ -124,6 +127,11 @@
         pl.semaphore_signal(barrier, inc=1, device_id=target, device_id_type=MESH)
 
     pairs = [
+        (nbr_ids_hbm, nbr_ref),
+        (mirror_hbm, mirror_ref),
+        (noise_hbm, noise_ref),
+        (node_hbm, node_ref),
+        (noisy_hbm, noisy_ref),
         (edge_hbm, raw),
         (time_embed_hbm, time_embed),
         (time_layer_hbm, time_layer),
@@ -134,6 +142,8 @@
     loads = [pltpu.make_async_copy(s, t, copy_sem.at[i]) for i, (s, t) in enumerate(pairs)]
     for load in loads:
         load.start()
+    for load in loads[:5]:
+        load.wait()
 
     def node_copy(layer, d, source):
         return pltpu.make_async_remote_copy(
@@ -175,13 +185,13 @@
     hist[0] = node_ref[...]
     for wide in wides:
         wide[pl.ds(2 * ROWS, 8)] = jnp.zeros((8, HALF), F32)
-    noise_high, noise_low = split(noise_ref[...])
+    noise_high, noise_low = split(0.5 * noise_ref[...])
     which = lax.broadcasted_iota(jnp.int32, (CITIES, WIDTH), 0)
     noise_rows = jnp.where(which < 2, noise_high, jnp.where(which == 2, noise_low, 0.0))
     picked_from[pl.ds(704, 64), pl.ds(0, WIDTH)] = noise_rows.astype(BF16)
     picked_from[pl.ds(576, 192), pl.ds(WIDTH, WIDTH)] = jnp.zeros((192, WIDTH), BF16)
 
-    loads[0].wait()
+    loads[5].wait()
 
     def widen(ch, carry):
         at = pl.multiple_of(ch * CHUNK, CHUNK)
@@ -190,21 +200,27 @@
 
     lax.fori_loop(0, CHUNKS, widen, 0)
 
-    def send_edges(l):
+    def send_exchange(l):
         for d in range(8):
             for p in range(CAP):
                 at = send_at[d, p]
                 to = (d * CAP + p) * 2
                 sent_wide[pl.ds(to, 1), :] = wides[l][pl.ds(at, 1), :]
                 sent_wide[pl.ds(to + 1, 1), :] = wides[l][pl.ds(at + 1, 1), :]
+        for d in range(8):
+            node_copy(l, d, hist.at[l] if l else node_ref).start()
         edges_sent[l] = halves(sent_wide, 0, INCOMING).astype(BF16)
         for d in range(8):
             edge_copy(l, d).start()
 
+    loads[6].wait()
+    loads[7].wait()
+    hidden = jnp.maximum(exact_dot(emb_ref[...], time_embed[...]), 0.0)
+    for l in range(LAYERS):
+        time_rows[pl.ds(8 * l, 8)] = exact_dot(hidden, time_layer[l])
+
     pl.semaphore_wait(barrier, 8)
-    for d in range(8):
-        node_copy(0, d, node_ref).start()
-    send_edges(0)
+    send_exchange(0)
 
     def gather_slot(l, k):
         for c in range(CITIES):
@@ -219,11 +235,9 @@
     rows = lax.broadcasted_iota(jnp.int32, (CITIES, HALF), 0)
     zero = jnp.zeros((CITIES, HALF), BF16)
 
-    def build(k, carry):
+    def build_slot(k, packed, noise):
         at = pl.ds(pl.multiple_of(k * CITIES, CITIES), CITIES)
-        packed = column(fields[pl.ds(k, 1)], eye).astype(jnp.int32)
-        noise = column(noisy_ref[pl.ds(k, 1)], eye)
-        packed = jnp.broadcast_to(packed, (CITIES, HALF))
+        packed = jnp.broadcast_to(packed.astype(jnp.int32), (CITIES, HALF))
         pick_at = (packed >> 8) - 1
         far_at = (packed & 255) - 1
         live = jnp.where(pick_at >= 0, 1.0, 0.0)
@@ -243,75 +257,91 @@
         live = live.astype(BF16)
         own_0[at, pl.ds(0, HALF)] = raw[at, pl.ds(0, HALF)] * live
         own_0[at, pl.ds(HALF, HALF)] = raw[at, pl.ds(HALF, HALF)] * live
-        gather_slot(0, k)
+
+    def build(g, carry):
+        slots = [g * GROUP + step for step in range(GROUP)]
+        found = [(column(fields[pl.ds(k, 1)], eye), column(noisy_ref[pl.ds(k, 1)], eye)) for k in slots]
+        for k, (packed, noise) in zip(slots, found):
+            build_slot(k, packed, noise)
+        for k in slots:
+            gather_slot(0, k)
         return carry
 
-    lax.fori_loop(0, SLOTS, build, 0)
-
-    for load in loads[1:]:
+    lax.fori_loop(0, SLOTS // GROUP, build, 0)
+
+    for load in loads[8:]:
         load.wait()
-    hidden = jnp.maximum(exact_dot(emb_ref[...], time_embed[...]), 0.0)
     for l in range(LAYERS):
-        time_rows[pl.ds(8 * l, 8)] = exact_dot(hidden, time_layer[l])
+        edge_w[l] = edge_w[l] * jnp.asarray(0.25 / 2**l, BF16)
+
+    def project(nodes, l):
+        values = dot(nodes, nbr_w[l])
+        return jnp.concatenate([values[:, :WIDTH] * 0.5, values[:, WIDTH:]], axis=1).astype(BF16)
 
     for l in range(LAYERS):
-        if l > 0:
-
-            def gather(g, carry, l=l):
-                for step in range(GROUP):
-                    gather_slot(l, g * GROUP + step)
-                return carry
-
-            lax.fori_loop(0, SLOTS // GROUP, gather, 0)
+        ahead = CHUNKS if l == 0 else AHEAD
+
+        def gather(g, carry, l=l):
+            for step in range(GROUP):
+                gather_slot(l, g * GROUP + step)
+            return carry
+
+        def pick_chunk(ch):
+            at = pl.ds(pl.multiple_of(ch * CHUNK, CHUNK), CHUNK)
+            picked = dot(pick[at], picked_from[...])
+            pre_part[at] = picked[:, :WIDTH]
+            messages[at] = picked[:, WIDTH:]
+
+        def gather_and_pick(ch, carry, l=l):
+            pick_chunk(ch)
+            for step in range(CHUNK // CITIES):
+                gather_slot(l, (ch + AHEAD) * (CHUNK // CITIES) + step)
+            return carry
+
+        def pick_only(ch, carry):
+            pick_chunk(ch)
+            return carry
+
         nodes = hist[l]
         own = dot(nodes, own_w[l])
-        high, low = split(own[:, :WIDTH] + time_rows[pl.ds(8 * l, 1)])
+        high, low = split(0.5 * (own[:, :WIDTH] + time_rows[pl.ds(8 * l, 1)]))
         picked_from[pl.ds(576, 64), pl.ds(0, WIDTH)] = high.astype(BF16)
         picked_from[pl.ds(640, 64), pl.ds(0, WIDTH)] = low.astype(BF16)
-        picked_from[pl.ds(512, 64)] = dot(nodes, nbr_w[l]).astype(BF16)
+        picked_from[pl.ds(512, 64)] = project(nodes, l)
+        if l > 0:
+            lax.fori_loop(0, AHEAD * CHUNK // CITIES // GROUP, gather, 0)
         for d in range(8):
             node_copy(l, d, node_ref).wait_recv()
-        picked_from[pl.ds(0, 512)] = dot(nodes_in[l], nbr_w[l]).astype(BF16)
+        picked_from[pl.ds(0, 512)] = project(nodes_in[l], l)
+        lax.fori_loop(0, CHUNKS - ahead, gather_and_pick, 0)
+        lax.fori_loop(CHUNKS - ahead, CHUNKS, pick_only, 0)
         for d in range(8):
             edge_copy(l, d).wait_recv()
 
-        def multiply(ch, l=l):
-            start = pl.multiple_of(ch * CHUNK, CHUNK)
-            at = pl.ds(start, CHUNK)
-            partner = halves(gathered, start, CHUNK) + dot(reach[at], edges_in[l])
-            averaged = ((owns[l][at].astype(F32) + partner) * 0.5).astype(BF16)
-            picked = dot(pick[at], picked_from[...])
-            averaged_buf[...] = averaged
-            pre_buf[...] = picked[:, :WIDTH] + dot(averaged, edge_w[l])
-            message_buf[...] = picked[:, WIDTH:].astype(BF16)
-
-        def apply(ch, total, l=l):
-            start = pl.multiple_of(ch * CHUNK, CHUNK)
-            pre = pre_buf[...]
-            message = message_buf[...].astype(F32)
-            gated = message + jnp.tanh(0.5 * pre) * message
-            total = total + jnp.sum(gated.reshape(CHUNK // CITIES, CITIES, WIDTH), axis=0)
-            following = averaged_buf[...].astype(F32) + jnp.maximum(norm(pre), 0.0)
-            following = following.astype(BF16)
-            owns[l + 1][pl.ds(start, CHUNK)] = following
+        def late(ch, total, l=l):
+            start = pl.multiple_of(ch * LATE, LATE)
+            at = pl.ds(start, LATE)
+            mine = own_0[at].astype(F32) if l == 0 else halves(wides[l], start, LATE)
+            both = mine + halves(gathered, start, LATE) + dot(reach[at], edges_in[l])
+            pre = pre_part[at] + dot(both.astype(BF16), edge_w[l])
+            message = messages[at]
+            gated = message + jnp.tanh(pre) * message
+            total = total + jnp.sum(gated.reshape(LATE // CITIES, CITIES, WIDTH), axis=0)
+            centered = pre - jnp.mean(pre, axis=-1, keepdims=True)
+            spread = jnp.sum(centered * centered, axis=-1, keepdims=True)
+            scale = lax.rsqrt(spread + 0.25e-05 * WIDTH) * (WIDTH**0.5 * 2 ** (l + 1))
+            following = both + jnp.maximum(centered * scale, 0.0)
             if l + 1 < LAYERS:
-                put_halves(wides[l + 1], start, following.astype(F32))
+                put_halves(wides[l + 1], start, following)
+            else:
+                own_3[at] = (following * 0.5 ** (l + 1)).astype(BF16)
             return total
 
-        def both(ch, total):
-            total = apply(ch - 1, total)
-            multiply(ch)
-            return total
-
-        multiply(0)
-        total = lax.fori_loop(1, CHUNKS, both, jnp.zeros((CITIES, WIDTH), F32))
-        total = apply(CHUNKS - 1, total)
+        total = lax.fori_loop(0, ROWS // LATE, late, jnp.zeros((CITIES, WIDTH), F32))
         update = jnp.maximum(norm(own[:, WIDTH:] + 0.5 * total), 0.0)
         hist[l + 1] = (nodes.astype(F32) + update).astype(BF16)
         if l + 1 < LAYERS:
-            send_edges(l + 1)
-            for d in range(8):
-                node_copy(l + 1, d, hist.at[l + 1]).start()
+            send_exchange(l + 1)
 
     store = pltpu.make_async_copy(own_3, edge_out, copy_sem.at[0])
     store.start()
@@ -330,6 +360,10 @@
 def by_slot(row):
     city = row // SLOTS
     return (row - city * SLOTS) * CITIES + city
+
+
+def in_hbm(array):
+    return pltpu.with_memory_space_constraint(array, pltpu.HBM)
 
 
 def on_device(
@@ -356,7 +390,7 @@
     embedding = jnp.broadcast_to(embedding, (8, WIDTH))
     edge_rows = jnp.transpose(edge_state, (1, 0, 2)).reshape(ROWS, WIDTH)
     vmem = pl.BlockSpec(memory_space=pltpu.VMEM)
-    hbm = pl.BlockSpec(memory_space=pl.ANY)
+    hbm = pl.BlockSpec(memory_space=pltpu.HBM)
     smem = pl.BlockSpec(memory_space=pltpu.SMEM)
     nbr, mirror = neighbors.T, mirror_src.T
     itself = jnp.arange(ROWS, dtype=jnp.int32).reshape(SLOTS, CITIES)
@@ -369,9 +403,14 @@
             jax.ShapeDtypeStruct((CITIES, WIDTH), BF16),
             jax.ShapeDtypeStruct((ROWS, WIDTH), BF16),
         ),
-        in_specs=[vmem, hbm] + [vmem] * 3 + [smem] * 2 + [hbm] * 3 + [vmem] * 2 + [hbm] * 2,
-        out_specs=(vmem, hbm),
+        in_specs=[hbm] * 5 + [smem] * 2 + [hbm] * 4 + [vmem] + [hbm] * 2,
+        out_specs=(vmem, pl.BlockSpec(memory_space=pl.ANY)),
         scratch_shapes=[
+            pltpu.VMEM((CITIES, WIDTH), BF16),
+            pltpu.VMEM((SLOTS, CITIES), F32),
+            pltpu.VMEM((SLOTS, CITIES), jnp.int32),
+            pltpu.VMEM((SLOTS, CITIES), jnp.int32),
+            pltpu.VMEM((1, WIDTH), F32),
             pltpu.VMEM((LAYERS, WIDTH, 2 * WIDTH), BF16),
             pltpu.VMEM((LAYERS, WIDTH, 2 * WIDTH), BF16),
             pltpu.VMEM((LAYERS, WIDTH, WIDTH), BF16),
@@ -379,16 +418,15 @@
             pltpu.VMEM((LAYERS, WIDTH, WIDTH), F32),
             pltpu.VMEM((ROWS, WIDTH), BF16),
         ]
-        + [pltpu.VMEM((ROWS, WIDTH), BF16)] * 4
+        + [pltpu.VMEM((ROWS, WIDTH), BF16)] * 2
         + [pltpu.VMEM((2 * ROWS + 8, HALF), F32)] * 3
         + [
             pltpu.VMEM((2 * ROWS, HALF), F32),
             pltpu.VMEM((ROWS, PICK), BF16),
             pltpu.VMEM((ROWS, INCOMING), BF16),
             pltpu.VMEM((PICK, 2 * WIDTH), BF16),
-            pltpu.VMEM((CHUNK, WIDTH), F32),
-            pltpu.VMEM((CHUNK, WIDTH), BF16),
-            pltpu.VMEM((CHUNK, WIDTH), BF16),
+            pltpu.VMEM((ROWS, WIDTH), F32),
+            pltpu.VMEM((ROWS, WIDTH), F32),
             pltpu.VMEM((SLOTS, CITIES), F32),
             pltpu.VMEM((2 * INCOMING, HALF), F32),
             pltpu.VMEM((8 * LAYERS, WIDTH), F32),
@@ -398,26 +436,28 @@
             pltpu.VMEM((LAYERS, INCOMING, WIDTH), BF16),
             pltpu.SemaphoreType.DMA((LAYERS, 16)),
             pltpu.SemaphoreType.DMA((LAYERS, 16)),
-            pltpu.SemaphoreType.DMA((8,)),
+            pltpu.SemaphoreType.DMA((11,)),
         ],
         compiler_params=pltpu.CompilerParams(
-            collective_id=0, has_side_effects=True, vmem_limit_bytes=44 * 1024 * 1024
+            collective_id=0, has_side_effects=True, vmem_limit_bytes=48 * 1024 * 1024
         ),
     )(
-        node_state,
-        edge_rows,
-        noisy_edges.T,
-        nbr,
-        mirror,
+        *map(
+            in_hbm,
+            (
+                node_state,
+                edge_rows,
+                noisy_edges.T,
+                nbr,
+                mirror,
+            ),
+        ),
         row_at,
         send_at,
-        node_own,
-        node_nbr,
-        edge_weight,
-        noise_embed[None, :],
+        *map(in_hbm, (node_own, node_nbr, edge_weight, noise_embed[None, :])),
         embedding,
-        time_embed,
-        time_layer,
+        in_hbm(time_embed),
+        in_hbm(time_layer),
     )
     edge_out = edge_out.reshape(SLOTS, CITIES, WIDTH)
     return (node_out, jnp.transpose(edge_out, (1, 0, 2)))

time: 64 us -> 53.4 us (0.83)
  local copies, waits for them, and re-layouts: 12.2 us -> 1.78 us
    unnamed x24 -> x2, local copies, waits for them, and re-layouts: 12.2 us -> 1.78 us
where the time goes in v3:
time: 53.4 us; the launch traced here: 53.2 us
  Pallas kernels  48.5 us (91%)
  local copies, waits for them, and re-layouts  1.78 us (3%)
  other arithmetic  1.57 us (3%)
  between operations  1.31 us (2%)
    pallas_call x1, Pallas kernels, on_device(): pl.pallas_call(functools.partial(kernel, grid_y, grid_x), out_shape=(jax....  48.5 us
    unnamed x2, local copies, waits for them, and re-layouts  1.78 us

profile of v3, /device:TPU:1, one launch (start us, length us, event | category | flops | bytes accessed | tf_op | source)
XLA Modules:
  0.0 53.2 jit_solution(636682413405407514)
XLA Ops:
  1.3 0.7 %fusion.6.send_at = s32[8,16]{1,0:T(8,128)S(1)} fusion(s32[1,8,16]{2,1,0:T(8,128)} %param.19), kind=kLoop, calls=%fused_computation.16 | loop fusion | flops 1920 | bytes 1024 | tf_op jit(solution)/shard_map/mul | solution.py:399
  2.1 0.8 %select_multiply_fusion.row_at = s32[50,64]{1,0:T(8,128)S(1)} fusion(s32[64,50]{0,1:T(8,128)} %param.18, s32[64,50]{0,1:T(8,128)} %param.17), kind=kLoop, calls=%fused_computation.1 | loop fusion | flops 67200 | bytes 38400 | tf_op jit(solution)/shard_map/mul | solution.py:398
  2.9 48.5 %shard_map.140 = (bf16[64,256]{1,0:T(8,128)(2,1)S(1)}, bf16[3200,256]{1,0:T(8,128)(2,1)S(1)}) custom-call(bf16[64,256]{1,0:T(8,128)(2,1)} %node_hbm.1, bf16[3200,256]{1,0:T(8,128)(2,1)} %bitcast.44, f32[50,64]{1,0:T(8,128)} %bitcast.47, s32[50,64]{1,0:T(8,128)} %bitcast.45, s32[50,64]{1,0:T(8,128)} %bitcast.46, s32[50,64]{1,0:T(8,128)S(1)} %select_multiply_fusion.row_at, ...), custom_call_target="tpu_custom_call" | custom-call | tf_op jit(solution)/shard_map/pallas_call | solution.py:400
  51.4 0.6 %copy.18 = bf16[64,256]{1,0:T(8,128)(2,1)} copy(bf16[64,256]{1,0:T(8,128)(2,1)S(1)} %get-tuple-element.10) | data formatting | bytes 65536
  52.0 1.2 %copy.19 = bf16[64,50,256]{2,0,1:T(8,128)(2,1)} copy(bf16[64,50,256]{2,0,1:T(8,128)(2,1)S(1)} %bitcast.43) | data formatting | bytes 3276800
  (3 shorter events, 0.1 us)

commit v4 on v3

--- a/solution.py
+++ b/solution.py
@@ -20,8 +20,7 @@
 CHUNK = 640
 CHUNKS = ROWS // CHUNK
 GROUP = 2
-AHEAD = 2
-LATE = 1600
+FAR = 512
 MESH = pl.DeviceIdType.MESH
 F32 = jnp.float32
 BF16 = jnp.bfloat16
@@ -104,6 +103,9 @@
     picked_from,
     pre_part,
     messages,
+    pre_buf,
+    message_buf,
+    both_buf,
     fields,
     sent_wide,
     time_rows,
@@ -279,27 +281,13 @@
         return jnp.concatenate([values[:, :WIDTH] * 0.5, values[:, WIDTH:]], axis=1).astype(BF16)
 
     for l in range(LAYERS):
-        ahead = CHUNKS if l == 0 else AHEAD
-
-        def gather(g, carry, l=l):
-            for step in range(GROUP):
-                gather_slot(l, g * GROUP + step)
-            return carry
-
-        def pick_chunk(ch):
+        def pick_own(ch, carry, l=l):
             at = pl.ds(pl.multiple_of(ch * CHUNK, CHUNK), CHUNK)
-            picked = dot(pick[at], picked_from[...])
+            picked = dot(pick[at, pl.ds(FAR, PICK - FAR)], picked_from[pl.ds(FAR, PICK - FAR)])
             pre_part[at] = picked[:, :WIDTH]
             messages[at] = picked[:, WIDTH:]
-
-        def gather_and_pick(ch, carry, l=l):
-            pick_chunk(ch)
             for step in range(CHUNK // CITIES):
-                gather_slot(l, (ch + AHEAD) * (CHUNK // CITIES) + step)
-            return carry
-
-        def pick_only(ch, carry):
-            pick_chunk(ch)
+                gather_slot(l, ch * (CHUNK // CITIES) + step)
             return carry
 
         nodes = hist[l]
@@ -309,35 +297,50 @@
         picked_from[pl.ds(640, 64), pl.ds(0, WIDTH)] = low.astype(BF16)
         picked_from[pl.ds(512, 64)] = project(nodes, l)
         if l > 0:
-            lax.fori_loop(0, AHEAD * CHUNK // CITIES // GROUP, gather, 0)
+            lax.fori_loop(0, CHUNKS, pick_own, 0)
         for d in range(8):
             node_copy(l, d, node_ref).wait_recv()
         picked_from[pl.ds(0, 512)] = project(nodes_in[l], l)
-        lax.fori_loop(0, CHUNKS - ahead, gather_and_pick, 0)
-        lax.fori_loop(CHUNKS - ahead, CHUNKS, pick_only, 0)
         for d in range(8):
             edge_copy(l, d).wait_recv()
 
-        def late(ch, total, l=l):
-            start = pl.multiple_of(ch * LATE, LATE)
-            at = pl.ds(start, LATE)
-            mine = own_0[at].astype(F32) if l == 0 else halves(wides[l], start, LATE)
-            both = mine + halves(gathered, start, LATE) + dot(reach[at], edges_in[l])
-            pre = pre_part[at] + dot(both.astype(BF16), edge_w[l])
-            message = messages[at]
+        def multiply(ch, l=l):
+            start = pl.multiple_of(ch * CHUNK, CHUNK)
+            at = pl.ds(start, CHUNK)
+            mine = own_0[at].astype(F32) if l == 0 else halves(wides[l], start, CHUNK)
+            both = mine + halves(gathered, start, CHUNK) + dot(reach[at], edges_in[l])
+            both_buf[...] = both
+            depth = PICK if l == 0 else FAR
+            picked = dot(pick[at, pl.ds(0, depth)], picked_from[pl.ds(0, depth)])
+            pre = picked[:, :WIDTH] + dot(both.astype(BF16), edge_w[l])
+            message = picked[:, WIDTH:]
+            pre_buf[...] = pre if l == 0 else pre + pre_part[at]
+            message_buf[...] = message if l == 0 else message + messages[at]
+
+        def apply(ch, total, l=l):
+            start = pl.multiple_of(ch * CHUNK, CHUNK)
+            pre = pre_buf[...]
+            message = message_buf[...]
             gated = message + jnp.tanh(pre) * message
-            total = total + jnp.sum(gated.reshape(LATE // CITIES, CITIES, WIDTH), axis=0)
+            total = total + jnp.sum(gated.reshape(CHUNK // CITIES, CITIES, WIDTH), axis=0)
             centered = pre - jnp.mean(pre, axis=-1, keepdims=True)
             spread = jnp.sum(centered * centered, axis=-1, keepdims=True)
             scale = lax.rsqrt(spread + 0.25e-05 * WIDTH) * (WIDTH**0.5 * 2 ** (l + 1))
-            following = both + jnp.maximum(centered * scale, 0.0)
+            following = both_buf[...] + jnp.maximum(centered * scale, 0.0)
             if l + 1 < LAYERS:
                 put_halves(wides[l + 1], start, following)
             else:
-                own_3[at] = (following * 0.5 ** (l + 1)).astype(BF16)
+                own_3[pl.ds(start, CHUNK)] = (following * 0.5 ** (l + 1)).astype(BF16)
             return total
 
-        total = lax.fori_loop(0, ROWS // LATE, late, jnp.zeros((CITIES, WIDTH), F32))
+        def overlap(ch, total):
+            total = apply(ch - 1, total)
+            multiply(ch)
+            return total
+
+        multiply(0)
+        total = lax.fori_loop(1, CHUNKS, overlap, jnp.zeros((CITIES, WIDTH), F32))
+        total = apply(CHUNKS - 1, total)
         update = jnp.maximum(norm(own[:, WIDTH:] + 0.5 * total), 0.0)
         hist[l + 1] = (nodes.astype(F32) + update).astype(BF16)
         if l + 1 < LAYERS:
@@ -427,6 +430,9 @@
             pltpu.VMEM((PICK, 2 * WIDTH), BF16),
             pltpu.VMEM((ROWS, WIDTH), F32),
             pltpu.VMEM((ROWS, WIDTH), F32),
+        ]
+        + [pltpu.VMEM((CHUNK, WIDTH), F32)] * 3
+        + [
             pltpu.VMEM((SLOTS, CITIES), F32),
             pltpu.VMEM((2 * INCOMING, HALF), F32),
             pltpu.VMEM((8 * LAYERS, WIDTH), F32),

time: 53.4 us -> 48.4 us (0.906)
  Pallas kernels: 48.5 us -> 43.5 us
    pallas_call x1, Pallas kernels: 48.5 us -> 43.5 us  [on_device(): pl.pallas_call(functools.partial(kernel, grid_y, grid_x), out_shape=(jax....]
where the time goes in v4:
time: 48.4 us; the launch traced here: 48.1 us
  Pallas kernels  43.5 us (90%)
  local copies, waits for them, and re-layouts  1.78 us (4%)
  other arithmetic  1.57 us (3%)
  between operations  1.31 us (3%)
    pallas_call x1, Pallas kernels, on_device(): pl.pallas_call(functools.partial(kernel, grid_y, grid_x), out_shape=(jax....  43.5 us
    unnamed x2, local copies, waits for them, and re-layouts  1.78 us

profile of v4, /device:TPU:1, one launch (start us, length us, event | category | flops | bytes accessed | tf_op | source)
XLA Modules:
  0.0 48.1 jit_solution(17308038719820784404)
XLA Ops:
  1.3 0.7 %fusion.6.send_at = s32[8,16]{1,0:T(8,128)S(1)} fusion(s32[1,8,16]{2,1,0:T(8,128)} %param.19), kind=kLoop, calls=%fused_computation.16 | loop fusion | flops 1920 | bytes 1024 | tf_op jit(solution)/shard_map/mul | solution.py:402
  2.1 0.8 %select_multiply_fusion.row_at = s32[50,64]{1,0:T(8,128)S(1)} fusion(s32[64,50]{0,1:T(8,128)} %param.18, s32[64,50]{0,1:T(8,128)} %param.17), kind=kLoop, calls=%fused_computation.1 | loop fusion | flops 67200 | bytes 38400 | tf_op jit(solution)/shard_map/mul | solution.py:401
  2.9 43.5 %shard_map.140 = (bf16[64,256]{1,0:T(8,128)(2,1)S(1)}, bf16[3200,256]{1,0:T(8,128)(2,1)S(1)}) custom-call(bf16[64,256]{1,0:T(8,128)(2,1)} %node_hbm.1, bf16[3200,256]{1,0:T(8,128)(2,1)} %bitcast.44, f32[50,64]{1,0:T(8,128)} %bitcast.47, s32[50,64]{1,0:T(8,128)} %bitcast.45, s32[50,64]{1,0:T(8,128)} %bitcast.46, s32[50,64]{1,0:T(8,128)S(1)} %select_multiply_fusion.row_at, ...), custom_call_target="tpu_custom_call" | custom-call | tf_op jit(solution)/shard_map/pallas_call | solution.py:403
  46.4 0.6 %copy.18 = bf16[64,256]{1,0:T(8,128)(2,1)} copy(bf16[64,256]{1,0:T(8,128)(2,1)S(1)} %get-tuple-element.10) | data formatting | bytes 65536
  47.0 1.2 %copy.19 = bf16[64,50,256]{2,0,1:T(8,128)(2,1)} copy(bf16[64,50,256]{2,0,1:T(8,128)(2,1)S(1)} %bitcast.43) | data formatting | bytes 3276800
  (3 shorter events, 0.1 us)

commit v5 on v4

--- a/solution.py
+++ b/solution.py
@@ -17,10 +17,12 @@
 CAP = 16
 INCOMING = 8 * CAP
 PICK = 768
-CHUNK = 640
+PART = 16
+CHUNK = PART * SLOTS
 CHUNKS = ROWS // CHUNK
 GROUP = 2
 FAR = 512
+EARLY = 640
 MESH = pl.DeviceIdType.MESH
 F32 = jnp.float32
 BF16 = jnp.bfloat16
@@ -71,7 +73,6 @@
     nbr_ids_hbm,
     mirror_hbm,
     row_at,
-    send_at,
     own_hbm,
     nbr_hbm,
     edge_w_hbm,
@@ -106,6 +107,7 @@
     pre_buf,
     message_buf,
     both_buf,
+    own_buf,
     fields,
     sent_wide,
     time_rows,
@@ -147,12 +149,14 @@
     for load in loads[:5]:
         load.wait()
 
-    def node_copy(layer, d, source):
+    def node_copy(layer, d, part=0):
+        start, count, source = (0, CITIES, node_ref) if layer == 0 else (part * PART, PART, hist.at[layer])
+        start = pl.multiple_of(start, count)
         return pltpu.make_async_remote_copy(
-            src_ref=source,
-            dst_ref=nodes_in.at[layer, pl.ds(d * CITIES, CITIES)],
-            send_sem=send_sem.at[layer, d],
-            recv_sem=recv_sem.at[layer, d],
+            src_ref=source.at[pl.ds(start, count)],
+            dst_ref=nodes_in.at[layer, pl.ds(d * CITIES + start, count)],
+            send_sem=send_sem.at[layer, 0],
+            recv_sem=recv_sem.at[layer, 0],
             device_id=targets[d],
             device_id_type=MESH,
         )
@@ -161,9 +165,20 @@
         return pltpu.make_async_remote_copy(
             src_ref=edges_sent.at[layer, pl.ds(d * CAP, CAP)],
             dst_ref=edges_in.at[layer, pl.ds(d * CAP, CAP)],
-            send_sem=send_sem.at[layer, 8 + d],
-            recv_sem=recv_sem.at[layer, 8 + d],
+            send_sem=send_sem.at[layer, 1],
+            recv_sem=recv_sem.at[layer, 1],
             device_id=targets[d],
+            device_id_type=MESH,
+        )
+
+    def all_copies(layer, kind):
+        block = (nodes_in, edges_in)[kind].at[layer]
+        return pltpu.make_async_remote_copy(
+            src_ref=block,
+            dst_ref=block,
+            send_sem=send_sem.at[layer, kind],
+            recv_sem=recv_sem.at[layer, kind],
+            device_id=targets[0],
             device_id_type=MESH,
         )
 
@@ -195,41 +210,50 @@
 
     loads[5].wait()
 
-    def widen(ch, carry):
-        at = pl.multiple_of(ch * CHUNK, CHUNK)
-        put_halves(wide_0, at, raw[pl.ds(at, CHUNK)].astype(F32))
+    def widen(g, carry):
+        for step in range(GROUP):
+            k = g * GROUP + step
+            values = raw[pl.ds(pl.multiple_of(k * CITIES, CITIES), CITIES)].astype(F32)
+            for part in range(CHUNKS):
+                put_halves(wide_0, part * CHUNK + k * PART, values[part * PART : (part + 1) * PART])
         return carry
 
-    lax.fori_loop(0, CHUNKS, widen, 0)
-
+    lax.fori_loop(0, SLOTS // GROUP, widen, 0)
     def send_exchange(l):
         for d in range(8):
             for p in range(CAP):
-                at = send_at[d, p]
+                at = row_at[SLOTS + d, p]
                 to = (d * CAP + p) * 2
                 sent_wide[pl.ds(to, 1), :] = wides[l][pl.ds(at, 1), :]
                 sent_wide[pl.ds(to + 1, 1), :] = wides[l][pl.ds(at + 1, 1), :]
-        for d in range(8):
-            node_copy(l, d, hist.at[l] if l else node_ref).start()
+        if l > 0:
+            for d in range(8):
+                node_copy(l, d, CHUNKS - 1).start()
         edges_sent[l] = halves(sent_wide, 0, INCOMING).astype(BF16)
         for d in range(8):
             edge_copy(l, d).start()
 
+    pl.semaphore_wait(barrier, 8)
+    for d in range(8):
+        node_copy(0, d).start()
+    send_exchange(0)
     loads[6].wait()
     loads[7].wait()
     hidden = jnp.maximum(exact_dot(emb_ref[...], time_embed[...]), 0.0)
     for l in range(LAYERS):
         time_rows[pl.ds(8 * l, 8)] = exact_dot(hidden, time_layer[l])
 
-    pl.semaphore_wait(barrier, 8)
-    send_exchange(0)
-
-    def gather_slot(l, k):
-        for c in range(CITIES):
-            at = row_at[k, c]
-            to = (k * CITIES + c) * 2
+
+    def gather_part(l, k, part, first):
+        for c in range(PART):
+            at = row_at[k, part * PART + c]
+            to = first + 2 * c
             gathered[pl.ds(to, 1), :] = wides[l][pl.ds(at, 1), :]
             gathered[pl.ds(to + 1, 1), :] = wides[l][pl.ds(at + 1, 1), :]
+
+    def gather_slot(l, k):
+        for part in range(CHUNKS):
+            gather_part(l, k, part, 2 * (part * CHUNK + k * PART))
 
     eye = lax.broadcasted_iota(jnp.int32, (CITIES, CITIES), 1)
     eye = eye == lax.broadcasted_iota(jnp.int32, (CITIES, CITIES), 0)
@@ -239,26 +263,33 @@
 
     def build_slot(k, packed, noise):
         at = pl.ds(pl.multiple_of(k * CITIES, CITIES), CITIES)
+        start = pl.multiple_of(k * PART, PART)
+
+        def put(ref, column, values):
+            for part in range(CHUNKS):
+                to = pl.ds(part * CHUNK + start, PART)
+                ref[to, pl.ds(column, HALF)] = values[part * PART : (part + 1) * PART]
+
         packed = jnp.broadcast_to(packed.astype(jnp.int32), (CITIES, HALF))
         pick_at = (packed >> 8) - 1
         far_at = (packed & 255) - 1
         live = jnp.where(pick_at >= 0, 1.0, 0.0)
-        reach[at] = jnp.where(lanes == far_at, 1.0, 0.0).astype(BF16)
+        put(reach, 0, jnp.where(lanes == far_at, 1.0, 0.0).astype(BF16))
         low = jnp.where(lanes == (pick_at & 127), 1.0, 0.0).astype(BF16)
         high = (pick_at >> 7).astype(F32).astype(BF16)
         hots = [jnp.where(high == jnp.asarray(t, BF16), low, zero) for t in range(5)]
         for t in range(4):
-            pick[at, pl.ds(t * HALF, HALF)] = hots[t]
+            put(pick, t * HALF, hots[t])
         own = jnp.where(lanes == rows + CITIES, live, 0.0)
-        pick[at, pl.ds(512, HALF)] = hots[4] + own.astype(BF16)
+        put(pick, 512, hots[4] + own.astype(BF16))
         noise_high, noise_low = split(noise * live)
         rest = jnp.where(lanes == rows, live, 0.0)
         rest = jnp.where((lanes == 64) | (lanes == 66), noise_high, rest)
         rest = jnp.where(lanes == 65, noise_low, rest)
-        pick[at, pl.ds(640, HALF)] = rest.astype(BF16)
+        put(pick, 640, rest.astype(BF16))
         live = live.astype(BF16)
-        own_0[at, pl.ds(0, HALF)] = raw[at, pl.ds(0, HALF)] * live
-        own_0[at, pl.ds(HALF, HALF)] = raw[at, pl.ds(HALF, HALF)] * live
+        put(own_0, 0, raw[at, pl.ds(0, HALF)] * live)
+        put(own_0, HALF, raw[at, pl.ds(HALF, HALF)] * live)
 
     def build(g, carry):
         slots = [g * GROUP + step for step in range(GROUP)]
@@ -282,27 +313,26 @@
 
     for l in range(LAYERS):
         def pick_own(ch, carry, l=l):
-            at = pl.ds(pl.multiple_of(ch * CHUNK, CHUNK), CHUNK)
+            at = pl.ds(pl.multiple_of(ch * EARLY, EARLY), EARLY)
             picked = dot(pick[at, pl.ds(FAR, PICK - FAR)], picked_from[pl.ds(FAR, PICK - FAR)])
             pre_part[at] = picked[:, :WIDTH]
             messages[at] = picked[:, WIDTH:]
-            for step in range(CHUNK // CITIES):
-                gather_slot(l, ch * (CHUNK // CITIES) + step)
+            for step in range(EARLY // CITIES):
+                gather_slot(l, ch * (EARLY // CITIES) + step)
             return carry
 
         nodes = hist[l]
         own = dot(nodes, own_w[l])
+        own_buf[...] = own[:, WIDTH:]
         high, low = split(0.5 * (own[:, :WIDTH] + time_rows[pl.ds(8 * l, 1)]))
         picked_from[pl.ds(576, 64), pl.ds(0, WIDTH)] = high.astype(BF16)
         picked_from[pl.ds(640, 64), pl.ds(0, WIDTH)] = low.astype(BF16)
         picked_from[pl.ds(512, 64)] = project(nodes, l)
         if l > 0:
-            lax.fori_loop(0, CHUNKS, pick_own, 0)
-        for d in range(8):
-            node_copy(l, d, node_ref).wait_recv()
+            lax.fori_loop(0, ROWS // EARLY, pick_own, 0)
+        all_copies(l, 0).wait_recv()
         picked_from[pl.ds(0, 512)] = project(nodes_in[l], l)
-        for d in range(8):
-            edge_copy(l, d).wait_recv()
+        all_copies(l, 1).wait_recv()
 
         def multiply(ch, l=l):
             start = pl.multiple_of(ch * CHUNK, CHUNK)
@@ -317,12 +347,12 @@
             pre_buf[...] = pre if l == 0 else pre + pre_part[at]
             message_buf[...] = message if l == 0 else message + messages[at]
 
-        def apply(ch, total, l=l):
+        def apply(ch, l=l):
             start = pl.multiple_of(ch * CHUNK, CHUNK)
             pre = pre_buf[...]
             message = message_buf[...]
             gated = message + jnp.tanh(pre) * message
-            total = total + jnp.sum(gated.reshape(CHUNK // CITIES, CITIES, WIDTH), axis=0)
+            total = jnp.sum(gated.reshape(SLOTS, PART, WIDTH), axis=0)
             centered = pre - jnp.mean(pre, axis=-1, keepdims=True)
             spread = jnp.sum(centered * centered, axis=-1, keepdims=True)
             scale = lax.rsqrt(spread + 0.25e-05 * WIDTH) * (WIDTH**0.5 * 2 ** (l + 1))
@@ -330,19 +360,25 @@
             if l + 1 < LAYERS:
                 put_halves(wides[l + 1], start, following)
             else:
-                own_3[pl.ds(start, CHUNK)] = (following * 0.5 ** (l + 1)).astype(BF16)
-            return total
-
-        def overlap(ch, total):
-            total = apply(ch - 1, total)
+                following = (following * 0.5 ** (l + 1)).astype(BF16)
+                for k in range(SLOTS):
+                    to = pl.multiple_of(k * CITIES + ch * PART, PART)
+                    own_3[pl.ds(to, PART)] = following[k * PART : (k + 1) * PART]
+            cities = pl.ds(pl.multiple_of(ch * PART, PART), PART)
+            update = jnp.maximum(norm(own_buf[cities] + 0.5 * total), 0.0)
+            hist[l + 1, cities] = (hist[l, cities].astype(F32) + update).astype(BF16)
+
+        def overlap(ch, carry, l=l):
+            apply(ch - 1)
             multiply(ch)
-            return total
+            if l + 1 < LAYERS:
+                for d in range(8):
+                    node_copy(l + 1, d, ch - 1).start()
+            return carry
 
         multiply(0)
-        total = lax.fori_loop(1, CHUNKS, overlap, jnp.zeros((CITIES, WIDTH), F32))
-        total = apply(CHUNKS - 1, total)
-        update = jnp.maximum(norm(own[:, WIDTH:] + 0.5 * total), 0.0)
-        hist[l + 1] = (nodes.astype(F32) + update).astype(BF16)
+        lax.fori_loop(1, CHUNKS, overlap, 0)
+        apply(CHUNKS - 1)
         if l + 1 < LAYERS:
             send_exchange(l + 1)
 
@@ -350,19 +386,19 @@
     store.start()
     node_out[...] = hist[LAYERS]
 
-    def drain(l, carry):
-        for d in range(8):
-            node_copy(l, d, node_ref).wait_send()
-            edge_copy(l, d).wait_send()
-        return carry
-
-    lax.fori_loop(0, LAYERS, drain, 0)
+    for l in range(LAYERS):
+        all_copies(l, 0).wait_send()
+        all_copies(l, 1).wait_send()
     store.wait()
 
 
+def row_of(slot, city):
+    return (city >> 4) * CHUNK + slot * PART + (city & (PART - 1))
+
+
 def by_slot(row):
-    city = row // SLOTS
-    return (row - city * SLOTS) * CITIES + city
+    city = (row * 5243) >> 18
+    return row_of(row - city * SLOTS, city)
 
 
 def in_hbm(array):
@@ -396,17 +432,19 @@
     hbm = pl.BlockSpec(memory_space=pltpu.HBM)
     smem = pl.BlockSpec(memory_space=pltpu.SMEM)
     nbr, mirror = neighbors.T, mirror_src.T
-    itself = jnp.arange(ROWS, dtype=jnp.int32).reshape(SLOTS, CITIES)
+    slot = lax.broadcasted_iota(jnp.int32, (SLOTS, CITIES), 0)
+    itself = row_of(slot, lax.broadcasted_iota(jnp.int32, (SLOTS, CITIES), 1))
     partner_at = jnp.where(mirror >= 0, jnp.where(mirror >= ROWS, ROWS, by_slot(mirror)), itself)
     row_at = jnp.where(nbr >= 0, partner_at, ROWS) * 2
     send_at = jnp.where(send_rows[0] >= 0, by_slot(send_rows[0]), ROWS) * 2
+    row_at = jnp.concatenate([row_at, jnp.pad(send_at, ((0, 0), (0, CITIES - CAP)))])
     node_out, edge_out = pl.pallas_call(
         functools.partial(kernel, grid_y, grid_x),
         out_shape=(
             jax.ShapeDtypeStruct((CITIES, WIDTH), BF16),
             jax.ShapeDtypeStruct((ROWS, WIDTH), BF16),
         ),
-        in_specs=[hbm] * 5 + [smem] * 2 + [hbm] * 4 + [vmem] + [hbm] * 2,
+        in_specs=[hbm] * 5 + [smem] + [hbm] * 4 + [vmem] + [hbm] * 2,
         out_specs=(vmem, pl.BlockSpec(memory_space=pl.ANY)),
         scratch_shapes=[
             pltpu.VMEM((CITIES, WIDTH), BF16),
@@ -433,6 +471,7 @@
         ]
         + [pltpu.VMEM((CHUNK, WIDTH), F32)] * 3
         + [
+            pltpu.VMEM((CITIES, WIDTH), F32),
             pltpu.VMEM((SLOTS, CITIES), F32),
             pltpu.VMEM((2 * INCOMING, HALF), F32),
             pltpu.VMEM((8 * LAYERS, WIDTH), F32),
@@ -440,8 +479,8 @@
             pltpu.VMEM((LAYERS, 8 * CITIES, WIDTH), BF16),
             pltpu.VMEM((LAYERS, INCOMING, WIDTH), BF16),
             pltpu.VMEM((LAYERS, INCOMING, WIDTH), BF16),
-            pltpu.SemaphoreType.DMA((LAYERS, 16)),
-            pltpu.SemaphoreType.DMA((LAYERS, 16)),
+            pltpu.SemaphoreType.DMA((LAYERS, 2)),
+            pltpu.SemaphoreType.DMA((LAYERS, 2)),
             pltpu.SemaphoreType.DMA((11,)),
         ],
         compiler_params=pltpu.CompilerParams(
@@ -459,7 +498,6 @@
             ),
         ),
         row_at,
-        send_at,
         *map(in_hbm, (node_own, node_nbr, edge_weight, noise_embed[None, :])),
         embedding,
         in_hbm(time_embed),

time: 48.4 us -> 44.6 us (0.921)
  Pallas kernels: 43.5 us -> 39.5 us
    pallas_call x1, Pallas kernels: 43.5 us -> 39.5 us  [on_device(): pl.pallas_call(functools.partial(kernel, grid_y, grid_x), out_shape=(jax....]
where the time goes in v5:
time: 44.6 us; the launch traced here: 44.2 us
  Pallas kernels  39.5 us (89%)
  local copies, waits for them, and re-layouts  1.78 us (4%)
  other arithmetic  1.62 us (4%)
  between operations  1.32 us (3%)
    pallas_call x1, Pallas kernels, on_device(): pl.pallas_call(functools.partial(kernel, grid_y, grid_x), out_shape=(jax....  39.5 us
    unnamed x2, local copies, waits for them, and re-layouts  1.78 us

profile of v5, /device:TPU:1, one launch (start us, length us, event | category | flops | bytes accessed | tf_op | source)
XLA Modules:
  0.0 44.2 jit_solution(8022348049886922517)
XLA Ops:
  1.3 0.1 fusion.9
  1.4 0.7 %fusion.5 = s32[8,16]{1,0:T(8,128)S(1)} fusion(s32[1,8,16]{2,1,0:T(8,128)} %param.19), kind=kLoop, calls=%fused_computation.10 | loop fusion | flops 1664 | bytes 1024 | tf_op jit(solution)/shard_map/mul | solution.py:439
  2.1 0.8 %select_multiply_fusion = s32[50,64]{1,0:T(8,128)S(1)} fusion(s32[64]{0:T(128)S(1)} %get-tuple-element.6, s32[50]{0:T(128)S(1)} %iota_multiply_fusion, s32[64]{0:T(128)S(1)} %get-tuple-element.7, s32[64,50]{0,1:T(8,128)} %param.18, s32[64,50]{0,1:T(8,128)} %param.17), kind=kLoop, calls=%fused_computation.1 | loop fusion | flops 60800 | bytes 39112 | tf_op jit(solution)/shard_map/mul | solution.py:438
  2.9 39.5 %shard_map.140 = (bf16[64,256]{1,0:T(8,128)(2,1)S(1)}, bf16[3200,256]{1,0:T(8,128)(2,1)S(1)}) custom-call(bf16[64,256]{1,0:T(8,128)(2,1)} %node_hbm.1, bf16[3200,256]{1,0:T(8,128)(2,1)} %bitcast.40, f32[50,64]{1,0:T(8,128)} %bitcast.43, s32[50,64]{1,0:T(8,128)} %bitcast.41, s32[50,64]{1,0:T(8,128)} %bitcast.42, s32[58,64]{1,0:T(8,128)S(1)} %pad_add_fusion.row_at, ...), custom_call_target="tpu_custom_call" | custom-call | tf_op jit(solution)/shard_map/pallas_call | solution.py:441
  42.4 0.6 %copy.18 = bf16[64,256]{1,0:T(8,128)(2,1)} copy(bf16[64,256]{1,0:T(8,128)(2,1)S(1)} %get-tuple-element.12) | data formatting | bytes 65536
  43.1 1.2 %copy.19 = bf16[64,50,256]{2,0,1:T(8,128)(2,1)} copy(bf16[64,50,256]{2,0,1:T(8,128)(2,1)S(1)} %bitcast.39) | data formatting | bytes 3276800
  (5 shorter events, 0.0 us)

commit v6 on v5

--- a/solution.py
+++ b/solution.py
@@ -44,10 +44,6 @@
     return jnp.dot(a, b, preferred_element_type=F32)
 
 
-def exact_dot(a, b):
-    return jnp.dot(a, b, precision=lax.Precision.HIGHEST, preferred_element_type=F32)
-
-
 def column(row, eye):
     return jnp.sum(jnp.where(eye, jnp.broadcast_to(row, eye.shape), 0.0), axis=1, keepdims=True)
 
@@ -62,6 +58,15 @@
     count = values.shape[0]
     ref[pl.ds(start * 2, count, stride=2), :] = values[:, :HALF]
     ref[pl.ds(start * 2 + 1, count, stride=2), :] = values[:, HALF:]
+
+
+def row_of(slot, city):
+    return (city >> 4) * CHUNK + slot * PART + (city & (PART - 1))
+
+
+def by_slot(row):
+    city = (row * 5243) >> 18
+    return row_of(row - city * SLOTS, city)
 
 
 def kernel(
@@ -72,7 +77,7 @@
     noisy_hbm,
     nbr_ids_hbm,
     mirror_hbm,
-    row_at,
+    send_hbm,
     own_hbm,
     nbr_hbm,
     edge_w_hbm,
@@ -86,6 +91,7 @@
     noisy_ref,
     nbr_ref,
     mirror_ref,
+    send_ref,
     noise_ref,
     own_w,
     nbr_w,
@@ -109,6 +115,10 @@
     both_buf,
     own_buf,
     fields,
+    row_table,
+    send_table,
+    row_at,
+    send_at,
     sent_wide,
     time_rows,
     hist,
@@ -133,6 +143,7 @@
     pairs = [
         (nbr_ids_hbm, nbr_ref),
         (mirror_hbm, mirror_ref),
+        (send_hbm, send_ref),
         (noise_hbm, noise_ref),
         (node_hbm, node_ref),
         (noisy_hbm, noisy_ref),
@@ -146,7 +157,7 @@
     loads = [pltpu.make_async_copy(s, t, copy_sem.at[i]) for i, (s, t) in enumerate(pairs)]
     for load in loads:
         load.start()
-    for load in loads[:5]:
+    for load in loads[:6]:
         load.wait()
 
     def node_copy(layer, d, part=0):
@@ -199,6 +210,18 @@
     is_far = mirror >= ROWS
     far_at = jnp.where(valid & is_far & inside, mirror - ROWS, -1)
     fields[...] = ((far_at + 1) + (pick_at + 1) * 256).astype(F32)
+    slots = lax.broadcasted_iota(jnp.int32, (SLOTS, CITIES), 0)
+    itself = row_of(slots, lax.broadcasted_iota(jnp.int32, (SLOTS, CITIES), 1))
+    partner_at = jnp.where(mirror >= 0, jnp.where(is_far, ROWS, by_slot(mirror)), itself)
+    row_table[...] = jnp.where(valid, partner_at, ROWS) * 2
+    sends = send_ref[0]
+    send_table[...] = jnp.where(sends >= 0, by_slot(sends), ROWS) * 2
+    tables = [
+        pltpu.make_async_copy(row_table, row_at, copy_sem.at[12]),
+        pltpu.make_async_copy(send_table, send_at, copy_sem.at[13]),
+    ]
+    for table in tables:
+        table.start()
     hist[0] = node_ref[...]
     for wide in wides:
         wide[pl.ds(2 * ROWS, 8)] = jnp.zeros((8, HALF), F32)
@@ -208,7 +231,7 @@
     picked_from[pl.ds(704, 64), pl.ds(0, WIDTH)] = noise_rows.astype(BF16)
     picked_from[pl.ds(576, 192), pl.ds(WIDTH, WIDTH)] = jnp.zeros((192, WIDTH), BF16)
 
-    loads[5].wait()
+    loads[6].wait()
 
     def widen(g, carry):
         for step in range(GROUP):
@@ -222,7 +245,7 @@
     def send_exchange(l):
         for d in range(8):
             for p in range(CAP):
-                at = row_at[SLOTS + d, p]
+                at = send_at[d, p]
                 to = (d * CAP + p) * 2
                 sent_wide[pl.ds(to, 1), :] = wides[l][pl.ds(at, 1), :]
                 sent_wide[pl.ds(to + 1, 1), :] = wides[l][pl.ds(at + 1, 1), :]
@@ -233,16 +256,21 @@
         for d in range(8):
             edge_copy(l, d).start()
 
+    for table in tables:
+        table.wait()
     pl.semaphore_wait(barrier, 8)
     for d in range(8):
         node_copy(0, d).start()
     send_exchange(0)
-    loads[6].wait()
     loads[7].wait()
-    hidden = jnp.maximum(exact_dot(emb_ref[...], time_embed[...]), 0.0)
+    loads[8].wait()
+    wide_eye = lax.broadcasted_iota(jnp.int32, (WIDTH, WIDTH), 1)
+    wide_eye = wide_eye == lax.broadcasted_iota(jnp.int32, (WIDTH, WIDTH), 0)
+    embedded = column(emb_ref[0:1], wide_eye)
+    hidden = jnp.sum(time_embed[...] * embedded, axis=0, keepdims=True)
+    hidden = column(jnp.maximum(hidden, 0.0), wide_eye)
     for l in range(LAYERS):
-        time_rows[pl.ds(8 * l, 8)] = exact_dot(hidden, time_layer[l])
-
+        time_rows[pl.ds(8 * l, 1)] = jnp.sum(time_layer[l] * hidden, axis=0, keepdims=True)
 
     def gather_part(l, k, part, first):
         for c in range(PART):
@@ -302,10 +330,14 @@
 
     lax.fori_loop(0, SLOTS // GROUP, build, 0)
 
-    for load in loads[8:]:
+    for load in loads[9:]:
         load.wait()
     for l in range(LAYERS):
         edge_w[l] = edge_w[l] * jnp.asarray(0.25 / 2**l, BF16)
+
+    def store(ch):
+        part = pl.ds(pl.multiple_of(ch * PART, PART), PART)
+        return pltpu.make_async_copy(own_3.at[:, part], edge_out.at[:, part], copy_sem.at[ch])
 
     def project(nodes, l):
         values = dot(nodes, nbr_w[l])
@@ -361,9 +393,8 @@
                 put_halves(wides[l + 1], start, following)
             else:
                 following = (following * 0.5 ** (l + 1)).astype(BF16)
-                for k in range(SLOTS):
-                    to = pl.multiple_of(k * CITIES + ch * PART, PART)
-                    own_3[pl.ds(to, PART)] = following[k * PART : (k + 1) * PART]
+                part = pl.ds(pl.multiple_of(ch * PART, PART), PART)
+                own_3[:, part, :] = following.reshape(SLOTS, PART, WIDTH)
             cities = pl.ds(pl.multiple_of(ch * PART, PART), PART)
             update = jnp.maximum(norm(own_buf[cities] + 0.5 * total), 0.0)
             hist[l + 1, cities] = (hist[l, cities].astype(F32) + update).astype(BF16)
@@ -374,6 +405,8 @@
             if l + 1 < LAYERS:
                 for d in range(8):
                     node_copy(l + 1, d, ch - 1).start()
+            else:
+                store(ch - 1).start()
             return carry
 
         multiply(0)
@@ -382,23 +415,14 @@
         if l + 1 < LAYERS:
             send_exchange(l + 1)
 
-    store = pltpu.make_async_copy(own_3, edge_out, copy_sem.at[0])
-    store.start()
+    store(CHUNKS - 1).start()
     node_out[...] = hist[LAYERS]
 
     for l in range(LAYERS):
         all_copies(l, 0).wait_send()
         all_copies(l, 1).wait_send()
-    store.wait()
-
-
-def row_of(slot, city):
-    return (city >> 4) * CHUNK + slot * PART + (city & (PART - 1))
-
-
-def by_slot(row):
-    city = (row * 5243) >> 18
-    return row_of(row - city * SLOTS, city)
+    for part in range(CHUNKS):
+        store(part).wait()
 
 
 def in_hbm(array):
@@ -430,27 +454,20 @@
     edge_rows = jnp.transpose(edge_state, (1, 0, 2)).reshape(ROWS, WIDTH)
     vmem = pl.BlockSpec(memory_space=pltpu.VMEM)
     hbm = pl.BlockSpec(memory_space=pltpu.HBM)
-    smem = pl.BlockSpec(memory_space=pltpu.SMEM)
-    nbr, mirror = neighbors.T, mirror_src.T
-    slot = lax.broadcasted_iota(jnp.int32, (SLOTS, CITIES), 0)
-    itself = row_of(slot, lax.broadcasted_iota(jnp.int32, (SLOTS, CITIES), 1))
-    partner_at = jnp.where(mirror >= 0, jnp.where(mirror >= ROWS, ROWS, by_slot(mirror)), itself)
-    row_at = jnp.where(nbr >= 0, partner_at, ROWS) * 2
-    send_at = jnp.where(send_rows[0] >= 0, by_slot(send_rows[0]), ROWS) * 2
-    row_at = jnp.concatenate([row_at, jnp.pad(send_at, ((0, 0), (0, CITIES - CAP)))])
     node_out, edge_out = pl.pallas_call(
         functools.partial(kernel, grid_y, grid_x),
         out_shape=(
             jax.ShapeDtypeStruct((CITIES, WIDTH), BF16),
-            jax.ShapeDtypeStruct((ROWS, WIDTH), BF16),
+            jax.ShapeDtypeStruct((SLOTS, CITIES, WIDTH), BF16),
         ),
-        in_specs=[hbm] * 5 + [smem] + [hbm] * 4 + [vmem] + [hbm] * 2,
+        in_specs=[hbm] * 10 + [vmem] + [hbm] * 2,
         out_specs=(vmem, pl.BlockSpec(memory_space=pl.ANY)),
         scratch_shapes=[
             pltpu.VMEM((CITIES, WIDTH), BF16),
             pltpu.VMEM((SLOTS, CITIES), F32),
             pltpu.VMEM((SLOTS, CITIES), jnp.int32),
             pltpu.VMEM((SLOTS, CITIES), jnp.int32),
+            pltpu.VMEM((1, 8, CAP), jnp.int32),
             pltpu.VMEM((1, WIDTH), F32),
             pltpu.VMEM((LAYERS, WIDTH, 2 * WIDTH), BF16),
             pltpu.VMEM((LAYERS, WIDTH, 2 * WIDTH), BF16),
@@ -459,7 +476,7 @@
             pltpu.VMEM((LAYERS, WIDTH, WIDTH), F32),
             pltpu.VMEM((ROWS, WIDTH), BF16),
         ]
-        + [pltpu.VMEM((ROWS, WIDTH), BF16)] * 2
+        + [pltpu.VMEM((ROWS, WIDTH), BF16), pltpu.VMEM((SLOTS, CITIES, WIDTH), BF16)]
         + [pltpu.VMEM((2 * ROWS + 8, HALF), F32)] * 3
         + [
             pltpu.VMEM((2 * ROWS, HALF), F32),
@@ -473,6 +490,10 @@
         + [
             pltpu.VMEM((CITIES, WIDTH), F32),
             pltpu.VMEM((SLOTS, CITIES), F32),
+            pltpu.VMEM((SLOTS, CITIES), jnp.int32),
+            pltpu.VMEM((8, CAP), jnp.int32),
+            pltpu.SMEM((SLOTS, CITIES), jnp.int32),
+            pltpu.SMEM((8, CAP), jnp.int32),
             pltpu.VMEM((2 * INCOMING, HALF), F32),
             pltpu.VMEM((8 * LAYERS, WIDTH), F32),
             pltpu.VMEM((LAYERS + 1, CITIES, WIDTH), BF16),
@@ -481,7 +502,7 @@
             pltpu.VMEM((LAYERS, INCOMING, WIDTH), BF16),
             pltpu.SemaphoreType.DMA((LAYERS, 2)),
             pltpu.SemaphoreType.DMA((LAYERS, 2)),
-            pltpu.SemaphoreType.DMA((11,)),
+            pltpu.SemaphoreType.DMA((14,)),
         ],
         compiler_params=pltpu.CompilerParams(
             collective_id=0, has_side_effects=True, vmem_limit_bytes=48 * 1024 * 1024
@@ -493,17 +514,16 @@
                 node_state,
                 edge_rows,
                 noisy_edges.T,
-                nbr,
-                mirror,
+                neighbors.T,
+                mirror_src.T,
+                send_rows,
             ),
         ),
-        row_at,
         *map(in_hbm, (node_own, node_nbr, edge_weight, noise_embed[None, :])),
         embedding,
         in_hbm(time_embed),
         in_hbm(time_layer),
     )
-    edge_out = edge_out.reshape(SLOTS, CITIES, WIDTH)
     return (node_out, jnp.transpose(edge_out, (1, 0, 2)))
 
 

time: 44.6 us -> 42.2 us (0.946)
  other arithmetic: 1.62 us -> 0.06 us
  Pallas kernels: 39.5 us -> 38.8 us
    mul x3 -> x0, other arithmetic: 1.55 us -> none  [the longest x1 0.84 us: on_device(): row_at = jnp.where(nbr >= 0, partner_at, ROWS) * 2]
    pallas_call x1, Pallas kernels: 39.5 us -> 38.8 us  [on_device(): pl.pallas_call(functools.partial(kernel, grid_y, grid_x), out_shape=(jax....]
where the time goes in v6:
time: 42.2 us; the launch traced here: 41.9 us
  Pallas kernels  38.8 us (92%)
  local copies, waits for them, and re-layouts  1.78 us (4%)
  between operations  1.3 us (3%)
    pallas_call x1, Pallas kernels, on_device(): pl.pallas_call(functools.partial(kernel, grid_y, grid_x), out_shape=(jax....  38.8 us
    unnamed x2, local copies, waits for them, and re-layouts  1.78 us

profile of v6, /device:TPU:1, one launch (start us, length us, event | category | flops | bytes accessed | tf_op | source)
XLA Modules:
  0.0 41.9 jit_solution(11147194059072371741)
XLA Ops:
  1.4 38.8 %shard_map.140 = (bf16[64,256]{1,0:T(8,128)(2,1)S(1)}, bf16[50,64,256]{2,1,0:T(8,128)(2,1)S(1)}) custom-call(bf16[64,256]{1,0:T(8,128)(2,1)} %node_hbm.1, bf16[3200,256]{1,0:T(8,128)(2,1)} %bitcast.10, f32[50,64]{1,0:T(8,128)} %bitcast.11, s32[50,64]{1,0:T(8,128)} %bitcast.12, s32[50,64]{1,0:T(8,128)} %bitcast.13, s32[1,8,16]{2,1,0:T(8,128)} %send_hbm.1, ...), custom_call_target="tpu_custom_call" | custom-call | tf_op jit(solution)/shard_map/pallas_call | solution.py:457
  40.1 0.6 %copy.18 = bf16[64,256]{1,0:T(8,128)(2,1)} copy(bf16[64,256]{1,0:T(8,128)(2,1)S(1)} %get-tuple-element.10) | data formatting | bytes 65536
  40.8 1.2 %copy.19 = bf16[64,50,256]{2,0,1:T(8,128)(2,1)} copy(bf16[64,50,256]{2,0,1:T(8,128)(2,1)S(1)} %bitcast.9) | data formatting | bytes 3276800
  (3 shorter events, 0.1 us)
